TPU v7x, 32 devices: a whole 2x2x4 slice. The times are simulated.
32 devices in a mesh: fsdp: 8 (over y, x, core), seq: 4 (over z).
Axes of the slice: x: 2, y: 2, z: 4, core: 2. Of those that a mesh axis runs over, the one named last changes fastest.
Arguments:
- inputs: bfloat16 [8192, 1536], P(('fsdp', 'seq')), may hold values from -6 to 6
- norm_attn: bfloat16 [1536], P('fsdp'), may hold values from 0.5 to 1.5
- w_proj: bfloat16 [1536, 6144], P('fsdp'), may hold values from -0.15625 to 0.15625
- w_small: bfloat16 [1536, 72], P('fsdp'), may hold values from -0.15625 to 0.15625
- forget_bias: float32 [24], replicated, may hold values from 3 to 9
- qk_gain: bfloat16 [2, 64], replicated, may hold values from 0.5 to 1.5
- w_out: bfloat16 [1536, 1536], P('fsdp'), may hold values from -0.625 to 0.625
- norm_ffn: bfloat16 [1536], P('fsdp'), may hold values from 0.5 to 1.5
- w_in: bfloat16 [1536, 8192], P('fsdp'), may hold values from -0.15625 to 0.15625
- w_down: bfloat16 [4096, 1536], P('fsdp'), may hold values from -0.09375 to 0.09375
- cotangent: bfloat16 [8192, 1536], P(('fsdp', 'seq')), may hold values from -6 to 6
Outputs:
- output: bfloat16 [8192, 1536], P(('fsdp', 'seq'))
- grad_inputs: float32 [8192, 1536], P(('fsdp', 'seq'))
- grad_norm_attn: float32 [1536], P('fsdp')
- grad_proj: float32 [1536, 6144], P('fsdp')
- grad_small: float32 [1536, 72], P('fsdp')
- grad_forget_bias: float32 [24], replicated
- grad_qk_gain: float32 [2, 64], replicated
- grad_out: float32 [1536, 1536], P('fsdp')
- grad_norm_ffn: float32 [1536], P('fsdp')
- grad_in: float32 [1536, 8192], P('fsdp')
- grad_down: float32 [4096, 1536], P('fsdp')
All inputs are finite; a program needn't handle non-finite values.
Results may differ from a plain program's by a relative error of at most 0.02.
Values may be sent and summed in bfloat16 or wider, within the bound.
No kernel may reach another device: no remote copies, remote signals or barrier semaphores. Data moves between devices by JAX's collectives and lax.ppermute only.
A program may use at most 320 MiB of HBM per device.

v0:
```python
from functools import partial

import jax
import jax.numpy as jnp
from jax import lax
from jax.sharding import PartitionSpec as P

QBLOCK = 512


epsilon = 1e-06
masked = -1e30


def product(left_side, right_side):
    return jnp.dot(left_side, right_side, preferred_element_type=jnp.float32)


def inner_rows(left_side, right_side):
    return lax.dot_general(
        left_side, right_side, (((0,), (0,)), ((), ())), preferred_element_type=jnp.float32
    )


def inner_cols(left_side, right_side):
    return lax.dot_general(
        left_side, right_side, (((1,), (1,)), ((), ())), preferred_element_type=jnp.float32
    )


def inverse_norm(values):
    return lax.rsqrt(jnp.mean(values * values, axis=-1, keepdims=True) + epsilon)


def norm_back(values, factor, grad_normed):
    normed = values * factor
    inner_mean = jnp.mean(grad_normed * normed, axis=-1, keepdims=True)
    return factor * (grad_normed - normed * inner_mean)


def shifted(values, mixing):
    earlier = jnp.concatenate([jnp.zeros_like(values[:1]), values[:-1]], axis=0)
    return ((1.0 - mixing)[..., None] * values + mixing[..., None] * earlier, earlier)


def shift_back(values, earlier, mixing, grad_mixed):
    carried = mixing[..., None] * grad_mixed
    following = jnp.concatenate([carried[1:], jnp.zeros_like(carried[:1])], axis=0)
    grad_values = (1.0 - mixing)[..., None] * grad_mixed + following
    grad_mixing = jnp.sum(grad_mixed * (earlier - values), axis=-1)
    return (grad_values, grad_mixing * mixing * (1.0 - mixing))


def heads_first(stacked):
    return jnp.moveaxis(stacked, 1, 0)


def block_scores(queries, key_rows, totals, block_start, score_scale):
    row_count = queries.shape[0]
    row_totals = lax.dynamic_slice_in_dim(totals, block_start, row_count, 0)
    scores = inner_cols(queries, key_rows) * score_scale + row_totals[:, None] - totals[None, :]
    query_index = block_start + lax.iota(jnp.int32, row_count)
    key_index = lax.iota(jnp.int32, key_rows.shape[0])
    return jnp.where(key_index[None, :] <= query_index[:, None], scores, masked)


def attend_head(head_item, block_rows, score_scale):
    queries, key_rows, value_rows, totals = head_item
    length = key_rows.shape[0]

    def one_block(block_start):
        query_block = lax.dynamic_slice_in_dim(queries, block_start, block_rows, 0)
        scores = block_scores(query_block, key_rows, totals, block_start, score_scale)
        row_max = jnp.max(scores, axis=1, keepdims=True)
        exponent = jnp.exp(scores - row_max)
        row_total = jnp.sum(exponent, axis=1, keepdims=True)
        probability = (exponent / row_total).astype(jnp.bfloat16)
        attended = product(probability, value_rows).astype(jnp.bfloat16)
        return (attended, row_max[:, 0] + jnp.log(row_total[:, 0]))

    starts = lax.iota(jnp.int32, length // block_rows) * block_rows
    attended, logsums = lax.map(one_block, starts)
    return (attended.reshape(length, value_rows.shape[1]), logsums.reshape(length))


def attend_back(head_item, block_rows, score_scale):
    queries, key_rows, value_rows, totals, logsums, grad_attended = head_item
    length, head_width = key_rows.shape

    def one_block(carried, block_start):
        grad_keys, grad_values, column_sums = carried
        query_block = lax.dynamic_slice_in_dim(queries, block_start, block_rows, 0)
        grad_block = lax.dynamic_slice_in_dim(grad_attended, block_start, block_rows, 0)
        logsum_block = lax.dynamic_slice_in_dim(logsums, block_start, block_rows, 0)
        scores = block_scores(query_block, key_rows, totals, block_start, score_scale)
        probability = jnp.exp(scores - logsum_block[:, None])
        grad_probability = inner_cols(grad_block, value_rows)
        grad_scores = probability * (
            grad_probability - jnp.sum(probability * grad_probability, axis=1, keepdims=True)
        )
        scores_low = grad_scores.astype(jnp.bfloat16)
        grad_queries = product(scores_low, key_rows) * score_scale
        grad_keys = grad_keys + inner_rows(scores_low, query_block) * score_scale
        grad_values = grad_values + inner_rows(probability.astype(jnp.bfloat16), grad_block)
        column_sums = column_sums + jnp.sum(grad_scores, axis=0)
        return ((grad_keys, grad_values, column_sums), (grad_queries, jnp.sum(grad_scores, axis=1)))

    initial = (
        jnp.zeros((length, head_width), jnp.float32),
        jnp.zeros((length, head_width), jnp.float32),
        jnp.zeros((length,), jnp.float32),
    )
    starts = lax.iota(jnp.int32, length // block_rows) * block_rows
    (grad_keys, grad_values, column_sums), (grad_queries, row_sums) = lax.scan(
        one_block, initial, starts
    )
    return (
        grad_queries.reshape(length, head_width),
        grad_keys,
        grad_values,
        row_sums.reshape(length) - column_sums,
    )


def body(
    inputs,
    norm_attn,
    w_proj,
    w_small,
    forget_bias,
    qk_gain,
    w_out,
    norm_ffn,
    w_in,
    w_down,
    cotangent,
):
    row_count, model_width = inputs.shape
    seq_parts = lax.axis_size("seq")
    head_count = forget_bias.shape[0]
    head_width = qk_gain.shape[1]
    local_heads = head_count // seq_parts
    length = row_count * seq_parts
    score_scale = head_width ** (-0.5)
    head_start = lax.axis_index("seq") * local_heads
    gain_attention, proj_full, small_full = (
        lax.all_gather(norm_attn, "fsdp", axis=0, tiled=True),
        lax.all_gather(w_proj, "fsdp", axis=0, tiled=True),
        lax.all_gather(w_small, "fsdp", axis=0, tiled=True),
    )
    out_full, gain_ffn, in_full, down_full = (
        lax.all_gather(w_out, "fsdp", axis=0, tiled=True),
        lax.all_gather(norm_ffn, "fsdp", axis=0, tiled=True),
        lax.all_gather(w_in, "fsdp", axis=0, tiled=True),
        lax.all_gather(w_down, "fsdp", axis=0, tiled=True),
    )
    hidden_width = in_full.shape[1] // 2
    source = inputs.astype(jnp.float32)
    factor_attention = inverse_norm(source)
    unit_attention = source * factor_attention
    normed = (unit_attention * gain_attention.astype(jnp.float32)).astype(jnp.bfloat16)
    projected = product(normed, proj_full).astype(jnp.bfloat16)
    logits_rows = product(normed, small_full).astype(jnp.bfloat16)
    head_proj, head_logits = (
        lax.all_to_all(
            projected.reshape(row_count, 4, model_width),
            "seq",
            split_axis=2,
            concat_axis=0,
            tiled=True,
        ),
        lax.all_to_all(
            logits_rows.reshape(row_count, 3, head_count),
            "seq",
            split_axis=2,
            concat_axis=0,
            tiled=True,
        ),
    )
    query_raw = head_proj[:, 0].astype(jnp.float32).reshape(length, local_heads, head_width)
    key_raw = head_proj[:, 1].astype(jnp.float32).reshape(length, local_heads, head_width)
    value_raw = head_proj[:, 2].astype(jnp.float32).reshape(length, local_heads, head_width)
    out_gate = head_proj[:, 3].astype(jnp.float32)
    logits = head_logits.astype(jnp.float32)
    norm_gains = qk_gain.astype(jnp.float32)
    factor_query = inverse_norm(query_raw)
    unit_query = query_raw * factor_query
    queries = (unit_query * norm_gains[0]).astype(jnp.bfloat16)
    factor_key = inverse_norm(key_raw)
    unit_key = key_raw * factor_key
    key_normed = unit_key * norm_gains[1]
    key_mix = jax.nn.sigmoid(logits[:, 1])
    value_mix = jax.nn.sigmoid(logits[:, 2])
    key_shifted, key_earlier = shifted(key_normed, key_mix)
    value_shifted, value_earlier = shifted(value_raw, value_mix)
    key_rows = key_shifted.astype(jnp.bfloat16)
    value_rows = value_shifted.astype(jnp.bfloat16)
    forget_logit = logits[:, 0] + lax.dynamic_slice_in_dim(forget_bias, head_start, local_heads, 0)
    totals = jnp.cumsum(jax.nn.log_sigmoid(forget_logit), axis=0)
    attended, logsums = lax.map(
        partial(attend_head, block_rows=QBLOCK, score_scale=score_scale),
        (heads_first(queries), heads_first(key_rows), heads_first(value_rows), totals.T),
    )
    attended = jnp.moveaxis(attended, 0, 1).reshape(length, local_heads * head_width)
    gate_sigmoid = jax.nn.sigmoid(out_gate)
    attended_wide = attended.astype(jnp.float32)
    gated_out = (attended_wide * gate_sigmoid).astype(jnp.bfloat16)
    mixed_rows = lax.all_to_all(gated_out, "seq", split_axis=0, concat_axis=1, tiled=True)
    residual = source + product(mixed_rows, out_full)
    factor_ffn = inverse_norm(residual)
    unit_ffn = residual * factor_ffn
    normed_ffn = (unit_ffn * gain_ffn.astype(jnp.float32)).astype(jnp.bfloat16)
    gate_up = product(normed_ffn, in_full)
    gate_part = gate_up[:, :hidden_width]
    up_part = gate_up[:, hidden_width:]
    inner_sigmoid = jax.nn.sigmoid(gate_part)
    silu_gate = gate_part * inner_sigmoid
    activated = (silu_gate * up_part).astype(jnp.bfloat16)
    output = (residual + product(activated, down_full)).astype(jnp.bfloat16)
    out_back, in_back, down_back = (
        lax.all_gather(w_out, "fsdp", axis=0, tiled=True),
        lax.all_gather(w_in, "fsdp", axis=0, tiled=True),
        lax.all_gather(w_down, "fsdp", axis=0, tiled=True),
    )
    grad_down = inner_rows(activated, cotangent)
    grad_act = inner_cols(cotangent, down_back)
    grad_gate = grad_act * up_part * inner_sigmoid * (1.0 + gate_part * (1.0 - inner_sigmoid))
    grad_up = grad_act * silu_gate
    grad_gate_up = jnp.concatenate([grad_gate, grad_up], axis=1).astype(jnp.bfloat16)
    grad_in = inner_rows(normed_ffn, grad_gate_up)
    grad_normed_ffn = inner_cols(grad_gate_up, in_back)
    grad_gain_ffn = jnp.sum(grad_normed_ffn * unit_ffn, axis=0)
    grad_residual = cotangent.astype(jnp.float32) + norm_back(
        residual, factor_ffn, grad_normed_ffn * gain_ffn.astype(jnp.float32)
    )
    grad_branch = grad_residual.astype(jnp.bfloat16)
    grad_out = inner_rows(mixed_rows, grad_branch)
    grad_mixed = inner_cols(grad_branch, out_back).astype(jnp.bfloat16)
    grad_heads = lax.all_to_all(grad_mixed, "seq", split_axis=1, concat_axis=0, tiled=True).astype(
        jnp.float32
    )
    grad_attended = (grad_heads * gate_sigmoid).astype(jnp.bfloat16)
    grad_gate_logit = grad_heads * attended_wide * gate_sigmoid * (1.0 - gate_sigmoid)
    grad_attended = heads_first(grad_attended.reshape(length, local_heads, head_width))
    grad_queries, grad_keys, grad_values, grad_totals = lax.map(
        partial(attend_back, block_rows=QBLOCK, score_scale=score_scale),
        (
            heads_first(queries),
            heads_first(key_rows),
            heads_first(value_rows),
            totals.T,
            logsums,
            grad_attended,
        ),
    )
    grad_queries = heads_first(grad_queries)
    grad_keys = heads_first(grad_keys)
    grad_values = heads_first(grad_values)
    grad_totals = grad_totals.T
    grad_forget = jnp.flip(jnp.cumsum(jnp.flip(grad_totals, axis=0), axis=0), axis=0) * (
        1.0 - jax.nn.sigmoid(forget_logit)
    )
    grad_key_normed, grad_key_mix = shift_back(key_normed, key_earlier, key_mix, grad_keys)
    grad_value_raw, grad_value_mix = shift_back(value_raw, value_earlier, value_mix, grad_values)
    grad_query_raw = norm_back(query_raw, factor_query, grad_queries * norm_gains[0])
    grad_key_raw = norm_back(key_raw, factor_key, grad_key_normed * norm_gains[1])
    grad_norm_gains = jnp.stack(
        [
            jnp.sum(grad_queries * unit_query, axis=(0, 1)),
            jnp.sum(grad_key_normed * unit_key, axis=(0, 1)),
        ]
    )
    grad_bias = lax.dynamic_update_slice_in_dim(
        jnp.zeros((head_count,), jnp.float32), jnp.sum(grad_forget, axis=0), head_start, 0
    )
    grad_proj_heads = jnp.stack(
        [
            grad_query_raw.reshape(length, -1),
            grad_key_raw.reshape(length, -1),
            grad_value_raw.reshape(length, -1),
            grad_gate_logit,
        ],
        axis=1,
    ).astype(jnp.bfloat16)
    grad_logits_heads = jnp.stack([grad_forget, grad_key_mix, grad_value_mix], axis=1).astype(
        jnp.bfloat16
    )
    grad_proj_rows, grad_logits_rows = (
        lax.all_to_all(grad_proj_heads, "seq", split_axis=0, concat_axis=2, tiled=True),
        lax.all_to_all(grad_logits_heads, "seq", split_axis=0, concat_axis=2, tiled=True),
    )
    grad_proj_rows = grad_proj_rows.reshape(row_count, 4 * model_width)
    grad_logits_rows = grad_logits_rows.reshape(row_count, 3 * head_count)
    grad_proj = inner_rows(normed, grad_proj_rows)
    grad_small = inner_rows(normed, grad_logits_rows)
    proj_piece = lax.all_gather(w_proj, "fsdp", axis=0, tiled=True)
    small_piece = lax.all_gather(w_small, "fsdp", axis=0, tiled=True)
    column_block = inner_cols(grad_proj_rows, proj_piece) + inner_cols(
        grad_logits_rows, small_piece
    )
    grad_gain_attention = jnp.sum(column_block * unit_attention, axis=0)
    grad_inputs = grad_residual + norm_back(
        source, factor_attention, column_block * gain_attention.astype(jnp.float32)
    )
    grad_qk_gain, grad_forget_bias = lax.psum((grad_norm_gains, grad_bias), ("fsdp", "seq"))
    piece_a, piece_b, piece_c, piece_d, piece_e, piece_f, piece_g = (
        lax.psum_scatter(
            grad_gain_attention.astype(jnp.bfloat16), "fsdp", scatter_dimension=0, tiled=True
        ).astype(jnp.float32),
        lax.psum_scatter(
            grad_proj.astype(jnp.bfloat16), "fsdp", scatter_dimension=0, tiled=True
        ).astype(jnp.float32),
        lax.psum_scatter(
            grad_small.astype(jnp.bfloat16), "fsdp", scatter_dimension=0, tiled=True
        ).astype(jnp.float32),
        lax.psum_scatter(
            grad_out.astype(jnp.bfloat16), "fsdp", scatter_dimension=0, tiled=True
        ).astype(jnp.float32),
        lax.psum_scatter(
            grad_gain_ffn.astype(jnp.bfloat16), "fsdp", scatter_dimension=0, tiled=True
        ).astype(jnp.float32),
        lax.psum_scatter(
            grad_in.astype(jnp.bfloat16), "fsdp", scatter_dimension=0, tiled=True
        ).astype(jnp.float32),
        lax.psum_scatter(
            grad_down.astype(jnp.bfloat16), "fsdp", scatter_dimension=0, tiled=True
        ).astype(jnp.float32),
    )
    shards = (
        lax.psum(piece_a.astype(jnp.bfloat16), "seq").astype(jnp.float32),
        lax.psum(piece_b.astype(jnp.bfloat16), "seq").astype(jnp.float32),
        lax.psum(piece_c.astype(jnp.bfloat16), "seq").astype(jnp.float32),
        lax.psum(piece_d.astype(jnp.bfloat16), "seq").astype(jnp.float32),
        lax.psum(piece_e.astype(jnp.bfloat16), "seq").astype(jnp.float32),
        lax.psum(piece_f.astype(jnp.bfloat16), "seq").astype(jnp.float32),
        lax.psum(piece_g.astype(jnp.bfloat16), "seq").astype(jnp.float32),
    )
    return (
        output,
        grad_inputs,
        shards[0],
        shards[1],
        shards[2],
        grad_forget_bias,
        grad_qk_gain,
        shards[3],
        shards[4],
        shards[5],
        shards[6],
    )


def solution(mesh):
    in_specs = (
        P(("fsdp", "seq"), None),
        P("fsdp"),
        P("fsdp", None),
        P("fsdp", None),
        P(),
        P(),
        P("fsdp", None),
        P("fsdp"),
        P("fsdp", None),
        P("fsdp", None),
        P(("fsdp", "seq"), None),
    )
    out_specs = (
        P(("fsdp", "seq"), None),
        P(("fsdp", "seq"), None),
        P("fsdp"),
        P("fsdp", None),
        P("fsdp", None),
        P(),
        P(),
        P("fsdp", None),
        P("fsdp"),
        P("fsdp", None),
        P("fsdp", None),
    )
    return jax.shard_map(body, mesh=mesh, in_specs=in_specs, out_specs=out_specs, check_vma=False)
```

profile of v0, /device:TPU:0, one launch (start us, length us, event | category | flops | bytes accessed | tf_op | source)
XLA Modules:
  0.0 1387.1 jit_solution(1758348870156208093)
XLA Ops:
  11.2 15.5 %all-reduce.10 = (bf16[1536]{0:T(1024)(128)(2,1)S(1)}, bf16[1536]{0:T(1024)(128)(2,1)S(1)}) all-reduce(bf16[1536]{0:T(1024)(128)(2,1)S(1)} %dynamic-update-slice, bf16[1536]{0:T(1024)(128)(2,1)S(1)} %dynamic-update-slice.1), channel_id=1, replica_groups=mesh['fsdp'=8,'seq'=4] {'fsdp'}, use_global_device_ids=true, to_apply=%add.4 | all-reduce | flops 3072 | bytes 12288
  26.8 9.7 all-gather
  38.2 4.9 all-to-all-start.1
  43.1 69.5 %all-gather.6.cloned.1.call-done = bf16[1536,6144]{1,0:T(8,128)(2,1)} async-done(((bf16[192,6144]{1,0:T(8,128)(2,1)}), bf16[1536,6144]{1,0:T(8,128)(2,1)}) %all-gather.6.cloned.1.call-update) | async-done | bytes 18874384 | tf_op jit(solution)/shard_map/all_gather | solution.py:148
  112.5 13.0 convolution_convert_fusion.4
  125.5 7.4 reshape.262
  132.9 7.4 copy.142
  140.3 4.6 all-to-all-start
  149.8 66.6 %all-to-all-done = bf16[256,4,1536]{0,1,2:T(4,128)(2,1)} async-done(((bf16[256,4,1536]{0,1,2:T(4,128)(2,1)}), bf16[256,4,1536]{0,1,2:T(4,128)(2,1)}, u32[]{:S(2)}, u32[]{:S(2)}) %all-to-all-start) | async-done | bytes 3145760 | tf_op jit(solution)/shard_map/all_to_all | solution.py:165
  216.4 6.0 copy.211
  222.4 6.1 all_to_all.67
  245.0 86.3 %while.60 = (s32[]{:T(128)}, bf16[6,1024,64]{1,2,0:T(8,128)(2,1)}, f32[6,1024]{1,0:T(8,128)S(1)}, bf16[6,1024,64]{2,1,0:T(8,128)(2,1)}, f32[6,1024]{1,0:T(8,128)...) while((s32[]{:T(128)}, bf16[6,1024,64]{1,2,0:T(8,128)(2,1)}, ...), condition=%wide.region_10.11_spmd, body=%wide.region_5.10_spmd.sunk | while | flops 140017664 | bytes 8645040 | solution.py:200
  247.8 10.5 while.63
  262.2 10.5 while.63
  276.5 10.5 while.63
  290.9 10.5 while.63
  305.3 10.5 while.63
  319.7 10.5 while.63
  347.9 19.6 %all-to-all-done.2 = bf16[4,256,384]{1,2,0:T(8,128)(2,1)S(1)} async-done(((bf16[4,256,384]{1,2,0:T(8,128)(2,1)}), bf16[4,256,384]{1,2,0:T(8,128)(2,1)S(1)}, u32[]{:S(2)}, u32[]{:S(2)}) %all-to-all-start.2) | async-done | bytes 786464 | tf_op jit(solution)/shard_map/all_to_all | solution.py:208
  367.5 3.8 multiply_reduce_fusion.4
  371.4 14.2 %fusion.86 = f32[256,8192]{1,0:T(8,128)} fusion(bf16[1536,8192]{1,0:T(8,128)(2,1)} %all-gather.10.cloned.1.call-done, f32[256,1536]{1,0:T(8,128)S(1)} %get-tuple-element.515, f32[1536]{0:T(1024)S(1)} %convert_element_type.249, f32[256]{0:T(256)S(1)} %add_rsqrt_fusion.2), kind=kOutput, calls=%fused_computation.195 | convolution fusion | flops 6443630592 | bytes 35134464 | tf_op jit(solution)/shard_map/dot_general | solution.py:16
  385.6 10.4 multiply_convert_fusion.1
  396.0 13.9 multiply_reduce_fusion.1
  416.5 3.8 convolution_convert_fusion.6
  421.3 4.4 all-to-all-start.3
  427.3 6.4 convolution_convert_fusion.3
  433.8 11.5 all-to-all-done.3
  452.4 212.6 %while.62 = (s32[]{:T(128)}, f32[6,1024,64]{1,2,0:T(8,128)}, f32[6,1024,64]{1,2,0:T(8,128)}, f32[6,1024,64]{1,2,0:T(8,128)}, f32[6,1024]{1,0:T(8,128)S(1)}, /*in...) while((s32[]{:T(128)}, f32[6,1024,64]{1,2,0:T(8,128)}, ...), condition=%wide.region_19.20_spmd, body=%wide.region_13.19_spmd.sunk | while | flops 343246336 | bytes 31550164 | solution.py:245
  459.3 25.5 %while.64 = (s32[]{:T(128)}, f32[1024,64]{0,1:T(8,128)}, f32[1024,64]{0,1:T(8,128)S(1)}, f32[1024]{0:T(1024)S(1)}, f32[2,512,64]{1,2,0:T(8,128)}, /*index=5*/f32...) while((s32[]{:T(128)}, f32[1024,64]{0,1:T(8,128)}, ...), condition=%wide.region_18.18_spmd.clone, body=%wide.region_14.17_spmd.clone.sunk | while | flops 343245312 | bytes 20232496 | solution.py:114
  495.0 25.4 %while.64 = (s32[]{:T(128)}, f32[1024,64]{0,1:T(8,128)}, f32[1024,64]{0,1:T(8,128)S(1)}, f32[1024]{0:T(1024)S(1)}, f32[2,512,64]{1,2,0:T(8,128)}, /*index=5*/f32...) while((s32[]{:T(128)}, f32[1024,64]{0,1:T(8,128)}, ...), condition=%wide.region_18.18_spmd.clone, body=%wide.region_14.17_spmd.clone.sunk | while | flops 343245312 | bytes 20232496 | solution.py:114
  530.6 25.3 %while.64 = (s32[]{:T(128)}, f32[1024,64]{0,1:T(8,128)}, f32[1024,64]{0,1:T(8,128)S(1)}, f32[1024]{0:T(1024)S(1)}, f32[2,512,64]{1,2,0:T(8,128)}, /*index=5*/f32...) while((s32[]{:T(128)}, f32[1024,64]{0,1:T(8,128)}, ...), condition=%wide.region_18.18_spmd.clone, body=%wide.region_14.17_spmd.clone.sunk | while | flops 343245312 | bytes 20232496 | solution.py:114
  566.0 25.3 %while.64 = (s32[]{:T(128)}, f32[1024,64]{0,1:T(8,128)}, f32[1024,64]{0,1:T(8,128)S(1)}, f32[1024]{0:T(1024)S(1)}, f32[2,512,64]{1,2,0:T(8,128)}, /*index=5*/f32...) while((s32[]{:T(128)}, f32[1024,64]{0,1:T(8,128)}, ...), condition=%wide.region_18.18_spmd.clone, body=%wide.region_14.17_spmd.clone.sunk | while | flops 343245312 | bytes 20232496 | solution.py:114
  601.3 25.3 %while.64 = (s32[]{:T(128)}, f32[1024,64]{0,1:T(8,128)}, f32[1024,64]{0,1:T(8,128)S(1)}, f32[1024]{0:T(1024)S(1)}, f32[2,512,64]{1,2,0:T(8,128)}, /*index=5*/f32...) while((s32[]{:T(128)}, f32[1024,64]{0,1:T(8,128)}, ...), condition=%wide.region_18.18_spmd.clone, body=%wide.region_14.17_spmd.clone.sunk | while | flops 343245312 | bytes 20232496 | solution.py:114
  636.7 25.3 %while.64 = (s32[]{:T(128)}, f32[1024,64]{0,1:T(8,128)}, f32[1024,64]{0,1:T(8,128)S(1)}, f32[1024]{0:T(1024)S(1)}, f32[2,512,64]{1,2,0:T(8,128)}, /*index=5*/f32...) while((s32[]{:T(128)}, f32[1024,64]{0,1:T(8,128)}, ...), condition=%wide.region_18.18_spmd.clone, body=%wide.region_14.17_spmd.clone.sunk | while | flops 343245312 | bytes 20232496 | solution.py:114
  681.0 73.8 %all_to_all.86 = bf16[1024,4,384]{2,1,0:T(4,128)(2,1)S(1)} all-to-all(bf16[1024,4,384]{2,1,0:T(4,128)(2,1)} %copy.162), channel_id=1, replica_groups=mesh['fsdp'=8,'seq'=4] {'seq'}, dimensions={0} | all-to-all | bytes 6291456 | tf_op jit(solution)/shard_map/all_to_all | solution.py:289
  756.9 4.7 copy.164
  761.6 11.1 convolution_convert_fusion.2
  774.1 19.2 %convolution_convert_fusion.1 = bf16[1536,8192]{1,0:T(8,128)(2,1)} fusion(bf16[256,4096]{1,0:T(8,128)(2,1)} %copy-done.33, bf16[256,4096]{1,0:T(8,128)(2,1)} %copy-done.32, f32[256,1536]{1,0:T(8,128)S(1)} %copy-done.6, f32[1536]{0:T(1024)S(1)} %copy-done.43, f32[256]{0:T(256)S(1)} %copy-done.57), kind=kOutput, calls=%fused_computation.52 | convolution fusion | flops 6464602112 | bytes 30940160 | tf_op jit(solution)/shard_map/dot_general | solution.py:20
  798.8 8.1 all_to_all.87
  810.0 87.2 %reduce-scatter.8.cloned.1.call-done = bf16[192,6144]{1,0:T(8,128)(2,1)} async-done(((bf16[1536,6144]{1,0:T(8,128)(2,1)}), bf16[192,6144]{1,0:T(8,128)(2,1)}) %reduce-scatter.8.cloned.1.call-update) | async-done | bytes 2359312 | tf_op jit(solution)/shard_map/reduce_scatter | solution.py:310
  897.2 161.0 %reduce-scatter.12.cloned.1.call-done = bf16[192,8192]{1,0:T(8,128)(2,1)} async-done(((bf16[1536,8192]{1,0:T(8,128)(2,1)}), bf16[192,8192]{1,0:T(8,128)(2,1)}) %reduce-scatter.12.cloned.1.call-update) | async-done | bytes 3145744 | tf_op jit(solution)/shard_map/reduce_scatter | solution.py:322
  1059.1 9.5 fusion.22
  1068.7 39.3 %all-reduce.8 = (f32[24]{0:T(128)}, f32[2,64]{1,0:T(2,128)}) all-reduce(f32[24]{0:T(128)S(1)} %dynamic_update_slice.39, f32[2,64]{1,0:T(2,128)S(1)} %pad_maximum_fusion.5), channel_id=1, replica_groups=mesh['fsdp'=8,'seq'=4] {'fsdp','seq'}, use_global_device_ids=true, to_apply=%region_35.36 | all-reduce | flops 152 | bytes 1216 | tf_op jit(solution)/shard_map/psum | solution.py:305
  1110.4 11.4 fusion.57
  1121.8 14.0 %all-reduce.9 = (bf16[1536]{0:T(1024)(128)(2,1)S(1)}, bf16[1536]{0:T(1024)(128)(2,1)S(1)}) all-reduce(bf16[1536]{0:T(1024)(128)(2,1)S(1)} %get-tuple-element.387, bf16[1536]{0:T(1024)(128)(2,1)S(1)} %copy-done.65), channel_id=2, replica_groups=mesh['fsdp'=8,'seq'=4] {'fsdp'}, use_global_device_ids=true, to_apply=%region_28.29.clone | all-reduce | flops 3072 | bytes 12288
  1136.0 25.8 %all-reduce.11 = (bf16[192]{0:T(256)(128)(2,1)S(1)}, bf16[192,72]{0,1:T(8,128)(2,1)S(1)}, bf16[192]{0:T(256)(128)(2,1)S(1)}) all-reduce(bf16[192]{0:T(256)(128)(2,1)S(1)} %dynamic-slice.3, bf16[192,72]{0,1:T(8,128)(2,1)S(1)} %copy.168, bf16[192]{0:T(256)(128)(2,1)S(1)} %dynamic-slice.5), channel_id=1, replica_groups=mesh['fsdp'=8,'seq'=4] {'seq'}, use_global_device_ids=true, to_apply=%region_29.30 | all-reduce | flops 14208 | bytes 56832 | tf_op jit(solution)/shard_map/psum | solution.py:330
  1166.5 202.1 %all-reduce.15.cloned.1.call-done = (bf16[192,6144]{1,0:T(8,128)(2,1)}, bf16[192,1536]{1,0:T(8,128)(2,1)}, bf16[192,8192]{1,0:T(8,128)(2,1)}, bf16[512,1536]{1,0:T(8,128)(2,1)}) async-done(((bf16[192,6144]{1,0:T(8,128)(2,1)}, bf16[192,1536]{1,0:T(8,128)(2,1)}, bf16[192,8192]{1,0:T(8,128)(2,1)}, bf16[512,1536]{1,0:T(8,128)(2,1)}), (bf16[192,6144]{1,0:T(8,128)(2,1)}, bf16[192,1536]{1,0:T(8,128)(2,1)}, ...) | async-done | bytes 7667728 | tf_op jit(solution)/shard_map/psum | solution.py:331
  1368.7 4.5 convert_element_type.267
  (782 shorter events, 354.1 us)
Async XLA Ops:
  7.2 105.3 %all-gather.6.cloned.1.call-start = ((), (), s32[]{:S(2)}) async-start(), calls=%async_computation.11 | async-start | bytes 21233664 | tf_op jit(solution)/shard_map/all_gather | solution.py:148
  7.9 340.0 %all-gather.8.cloned.1.call-start = ((), (), s32[]{:S(2)}) async-start(), calls=%async_computation.12 | async-start | bytes 5308416 | tf_op jit(solution)/shard_map/all_gather | solution.py:152
  8.7 18.1 %copy-start.58 = (bf16[192,72]{0,1:T(8,128)(2,1)S(1)}, bf16[192,72]{0,1:T(8,128)(2,1)}, u32[]{:S(2)}) copy-start(bf16[192,72]{0,1:T(8,128)(2,1)} %param.22) | copy-start | bytes 82948
  8.7 28.1 %copy-start.14 = (bf16[256,1536]{1,0:T(8,128)(2,1)S(1)}, bf16[256,1536]{1,0:T(8,128)(2,1)}, u32[]{:S(2)}) copy-start(bf16[256,1536]{1,0:T(8,128)(2,1)} %param.19) | copy-start | bytes 2359300
  8.7 362.7 %all-gather.10.cloned.1.call-start = ((), (), s32[]{:S(2)}) async-start(), calls=%async_computation.13 | async-start | bytes 28311552 | tf_op jit(solution)/shard_map/all_gather | solution.py:154
  26.8 85.8 %copy-start.52 = (f32[1536]{0:T(1024)}, f32[1536]{0:T(1024)S(1)}, u32[]{:S(2)}) copy-start(f32[1536]{0:T(1024)S(1)} %convert_element_type.226) | copy-start | bytes 18436
  36.8 88.7 %copy-start.37 = (bf16[1536,72]{0,1:T(8,128)(2,1)}, bf16[1536,72]{0,1:T(8,128)(2,1)S(1)}, u32[]{:S(2)}) copy-start(bf16[1536,72]{0,1:T(8,128)(2,1)S(1)} %reshape.290) | copy-start | bytes 663556
  37.1 88.4 %copy-start.59 = (f32[256]{0:T(256)}, f32[256]{0:T(256)S(1)}, u32[]{:S(2)}) copy-start(f32[256]{0:T(256)S(1)} %add_rsqrt_fusion.3) | copy-start | bytes 3076
  38.2 102.1 %all-to-all-start.1 = ((bf16[256,3,24]{0,1,2:T(4,128)(2,1)}), bf16[256,3,24]{0,1,2:T(4,128)(2,1)S(1)}, u32[]{:S(2)}, u32[]{:S(2)}) async-start(bf16[256,3,24]{0,1,2:T(4,128)(2,1)} %copy.145), calls=%async_computation.1 | async-start | bytes 98304 | tf_op jit(solution)/shard_map/all_to_all | solution.py:172
  140.3 76.1 %all-to-all-start = ((bf16[256,4,1536]{0,1,2:T(4,128)(2,1)}), bf16[256,4,1536]{0,1,2:T(4,128)(2,1)}, u32[]{:S(2)}, u32[]{:S(2)}) async-start(bf16[256,4,1536]{0,1,2:T(4,128)(2,1)} %copy.142), calls=%async_computation | async-start | bytes 6291456 | tf_op jit(solution)/shard_map/all_to_all | solution.py:165
  145.0 240.7 %all-gather.12.cloned.1.call-start = ((), (), s32[]{:S(2)}) async-start(), calls=%async_computation.14 | async-start | bytes 14155776 | tf_op jit(solution)/shard_map/all_gather | solution.py:155
  145.7 88.5 %copy-start.63 = (f32[64]{0:T(128)}, f32[64]{0:T(128)S(1)}, u32[]{:S(2)}) copy-start(f32[64]{0:T(128)S(1)} %get-tuple-element.511) | copy-start | bytes 772
  145.7 92.8 %copy-start.61 = (f32[64]{0:T(128)}, f32[64]{0:T(128)S(1)}, u32[]{:S(2)}) copy-start(f32[64]{0:T(128)S(1)} %get-tuple-element.510) | copy-start | bytes 772
  145.7 76.6 %copy-start.35 = (f32[256,3,4,6]{0,3,2,1:T(8,128)}, f32[256,3,4,6]{0,3,2,1:T(8,128)S(1)}, u32[]{:S(2)}) copy-start(f32[256,3,4,6]{0,3,2,1:T(8,128)S(1)} %reshape.282) | copy-start | bytes 221188
  146.4 92.1 %copy-start.47 = (f32[1024,6]{0,1:T(8,128)}, f32[1024,6]{0,1:T(8,128)S(1)}, u32[]{:S(2)}) copy-start(f32[1024,6]{0,1:T(8,128)S(1)} %get-tuple-element.506) | copy-start | bytes 73732
  149.8 88.7 %copy-start.50 = (f32[1024,6]{0,1:T(8,128)}, f32[1024,6]{0,1:T(8,128)S(1)}, u32[]{:S(2)}) copy-start(f32[1024,6]{0,1:T(8,128)S(1)} %get-tuple-element.509) | copy-start | bytes 73732
  231.1 7.4 copy-start.1
  343.9 23.6 %all-to-all-start.2 = ((bf16[4,256,384]{1,2,0:T(8,128)(2,1)}), bf16[4,256,384]{1,2,0:T(8,128)(2,1)S(1)}, u32[]{:S(2)}, u32[]{:S(2)}) async-start(bf16[4,256,384]{1,2,0:T(8,128)(2,1)} %copy.151), calls=%async_computation.2 | async-start | bytes 1572864 | tf_op jit(solution)/shard_map/all_to_all | solution.py:208
  347.4 462.6 %reduce-scatter.10.cloned.1.call-start = ((), (), s32[]{:S(2)}) async-start(), calls=%async_computation.16 | async-start | bytes 5308416 | tf_op jit(solution)/shard_map/reduce_scatter | solution.py:316
  347.9 62.0 %copy-start.42 = (f32[1536]{0:T(1024)}, f32[1536]{0:T(1024)S(1)}, u32[]{:S(2)}) copy-start(f32[1536]{0:T(1024)S(1)} %convert_element_type.249) | copy-start | bytes 18436
  371.3 38.6 %copy-start.5 = (f32[256,1536]{1,0:T(8,128)}, f32[256,1536]{1,0:T(8,128)S(1)}, u32[]{:S(2)}) copy-start(f32[256,1536]{1,0:T(8,128)S(1)} %get-tuple-element.515) | copy-start | bytes 4718596
  371.3 38.5 %copy-start.56 = (f32[256]{0:T(256)}, f32[256]{0:T(256)S(1)}, u32[]{:S(2)}) copy-start(f32[256]{0:T(256)S(1)} %add_rsqrt_fusion.2) | copy-start | bytes 3076
  371.4 14.3 %copy-start.26 = (bf16[256,1536]{1,0:T(8,128)(2,1)S(1)}, bf16[256,1536]{1,0:T(8,128)(2,1)}, u32[]{:S(2)}) copy-start(bf16[256,1536]{1,0:T(8,128)(2,1)} %param.29) | copy-start | bytes 2359300
  396.0 13.9 copy-start.32
  396.0 13.9 copy-start.33
  420.3 5.6 copy-start.51
  420.3 6.3 copy-start.49
  420.3 7.0 copy-start.25
  420.4 7.0 copy-start.27
  421.3 24.0 %all-to-all-start.3 = ((bf16[256,4,384]{2,0,1:T(8,128)(2,1)}), bf16[256,4,384]{2,0,1:T(8,128)(2,1)}, u32[]{:S(2)}, u32[]{:S(2)}) async-start(bf16[256,4,384]{2,0,1:T(8,128)(2,1)} %bitcast.312), calls=%async_computation.3 | async-start | bytes 1572864 | tf_op jit(solution)/shard_map/all_to_all | solution.py:239
  425.7 384.3 %reduce-scatter.14.cloned.1.call-start = ((), (), s32[]{:S(2)}) async-start(), calls=%async_computation.18 | async-start | bytes 14155776 | tf_op jit(solution)/shard_map/reduce_scatter | solution.py:325
  433.8 463.5 %reduce-scatter.8.cloned.1.call-start = ((), (), s32[]{:S(2)}) async-start(), calls=%async_computation.15 | async-start | bytes 21233664 | tf_op jit(solution)/shard_map/reduce_scatter | solution.py:310
  452.4 6.9 copy-start.30
  488.1 7.0 copy-start.30
  523.6 6.9 copy-start.30
  559.0 6.9 copy-start.30
  594.4 6.9 copy-start.30
  629.7 6.9 copy-start.30
  756.9 4.7 copy-start.15
  756.9 4.7 copy-start.53
  756.9 4.7 copy-start.60
  772.7 285.5 %reduce-scatter.12.cloned.1.call-start = ((), (), s32[]{:S(2)}) async-start(), calls=%async_computation.17 | async-start | bytes 28311552 | tf_op jit(solution)/shard_map/reduce_scatter | solution.py:322
  793.4 316.1 %reduce-scatter.16.cloned.1.call-start = ((), (), s32[]{:S(2)}) async-start(), calls=%async_computation.19 | async-start | bytes 442368
  809.7 559.0 %all-reduce.15.cloned.1.call-start = ((), (), s32[]{:S(2)}) async-start(), calls=%async_computation.20 | async-start | bytes 15335424 | tf_op jit(solution)/shard_map/psum | solution.py:331
  1059.1 48.8 %copy-start.38 = (bf16[1536,72]{0,1:T(8,128)(2,1)S(1)}, bf16[1536,72]{0,1:T(8,128)(2,1)}, u32[]{:S(2)}) copy-start(bf16[1536,72]{0,1:T(8,128)(2,1)} %copy-done.37) | copy-start | bytes 663556
  1110.4 11.4 copy-start.65
  1110.4 53.2 %copy-start.13 = (f32[256,1536]{1,0:T(8,128)S(1)}, f32[256,1536]{1,0:T(8,128)}, u32[]{:S(2)}) copy-start(f32[256,1536]{1,0:T(8,128)} %copy-done.11) | copy-start | bytes 4718596
  1368.7 5.7 copy-start.28
  (76 other events, 136.0 us)
Sparse Core Ops, SparseCore 0:
  9.9 102.5 all-gather.5
  114.4 38.9 all-gather.7
  155.2 125.3 all-gather.9
  282.3 72.1 all-gather.11
  415.2 52.0 reduce-scatter.9
  471.1 92.3 reduce-scatter.13
  772.9 124.3 reduce-scatter.7
  901.3 156.8 reduce-scatter.11
  1062.1 33.8 reduce-scatter.15
  1098.7 269.9 all-reduce.14
where the time goes:
time: 1400 us; the launch traced here: 1390 us
  waiting for transfers between devices  620 us (44%)
  matrix products  239 us (17%)
  local copies, waits for them, and re-layouts  188 us (13%)
  blocking collectives  186 us (13%)
  other arithmetic  72.2 us (5%)
  loops' own time  45.7 us (3%)
  starting transfers between devices  18.8 us (1%)
  between operations  16.9 us (1%)
    psum x1, waiting for transfers between devices, body(): lax.psum(piece_b.astype(jnp.bfloat16), 'seq').astype(jnp.float32)  202 us
    reduce_scatter x1, waiting for transfers between devices, body(): lax.psum_scatter(grad_in.astype(jnp.bfloat16), 'fsdp', scatter_dimension=...  161 us
    dot_general x41, matrix products, inner_cols(): lax.dot_general(left_side, right_side, (((1,), (1,)), ((), ())), preferre...  92.8 us
    reduce_scatter x1, waiting for transfers between devices, body(): lax.psum_scatter(grad_proj.astype(jnp.bfloat16), 'fsdp', scatter_dimensio...  87.2 us
    dot_general x29, matrix products, inner_rows(): lax.dot_general(left_side, right_side, (((0,), (0,)), ((), ())), preferre...  80.9 us
    all_to_all x1, blocking collectives, body(): lax.all_to_all(grad_proj_heads, 'seq', split_axis=0, concat_axis=2, tiled...  73.8 us
    all_gather x1, waiting for transfers between devices, body(): lax.all_gather(w_proj, 'fsdp', axis=0, tiled=True)  69.5 us
    all_to_all x1, waiting for transfers between devices, body(): lax.all_to_all(projected.reshape(row_count, 4, model_width), 'seq', split...  66.6 us
  transfers between devices with their start and end apart: 14, of which 7 were waited for; matrix products, arithmetic and copies ran while one was open for 32% of the time, Pallas kernels for 0%

commit v1 on v0

v1 whole, which is shorter than its diff:
```python
from functools import partial

import jax
import jax.numpy as jnp
from jax import lax
from jax.experimental import pallas as pl
from jax.experimental.pallas import tpu as pltpu
from jax.sharding import PartitionSpec as P

epsilon = 1e-06
LANES = 128
QROWS = 256


def dot_ab(a, b):
    return lax.dot_general(a, b, (((1,), (0,)), ((), ())), preferred_element_type=jnp.float32)


def dot_abt(a, b):
    return lax.dot_general(a, b, (((1,), (1,)), ((), ())), preferred_element_type=jnp.float32)


def dot_atb(a, b):
    return lax.dot_general(a, b, (((0,), (0,)), ((), ())), preferred_element_type=jnp.float32)


def lane_ids(rows):
    return lax.broadcasted_iota(jnp.int32, (rows, LANES), 1)


def row_ids(rows):
    return lax.broadcasted_iota(jnp.int32, (rows, LANES), 0)


def group_sum(values, block_ones):
    high = values.astype(jnp.bfloat16)
    low = (values - high.astype(jnp.float32)).astype(jnp.bfloat16)
    return dot_ab(high, block_ones) + dot_ab(low, block_ones)


def selector(first_column, half):
    column = lax.broadcasted_iota(jnp.int32, (LANES, LANES), 0)
    lane = lax.broadcasted_iota(jnp.int32, (LANES, LANES), 1)
    wanted = first_column + (lane >= half).astype(jnp.int32)
    return (column == wanted).astype(jnp.float32).astype(jnp.bfloat16)


def prepare(q_ref, k_ref, v_ref, small_ref, bias_ref, gain_ref, heads):
    length = q_ref.shape[0]
    half = LANES // 2
    pair = pl.program_id(0)
    row_block = lax.broadcasted_iota(jnp.int32, (LANES, LANES), 0) >= half
    lane_block = lax.broadcasted_iota(jnp.int32, (LANES, LANES), 1) >= half
    block_ones = (row_block == lane_block).astype(jnp.float32).astype(jnp.bfloat16)
    first_row = row_ids(length) == 0
    query = q_ref[...].astype(jnp.float32)
    key = k_ref[...].astype(jnp.float32)
    value = v_ref[...].astype(jnp.float32)
    small = small_ref[...]
    factor_query = lax.rsqrt(group_sum(query * query, block_ones) * (1.0 / half) + epsilon)
    factor_key = lax.rsqrt(group_sum(key * key, block_ones) * (1.0 / half) + epsilon)
    unit_query = query * factor_query
    unit_key = key * factor_key
    key_normed = unit_key * gain_ref[1:2, :]
    forget = dot_ab(small, selector(2 * pair, half)) + bias_ref[0]
    key_mix = jax.nn.sigmoid(dot_ab(small, selector(heads + 2 * pair, half)))
    value_mix = jax.nn.sigmoid(dot_ab(small, selector(2 * heads + 2 * pair, half)))
    key_earlier = jnp.where(first_row, 0.0, pltpu.roll(key_normed, 1, 0))
    value_earlier = jnp.where(first_row, 0.0, pltpu.roll(value, 1, 0))
    queries = (unit_query * gain_ref[0:1, :]).astype(jnp.bfloat16)
    keys = ((1.0 - key_mix) * key_normed + key_mix * key_earlier).astype(jnp.bfloat16)
    values = ((1.0 - value_mix) * value + value_mix * value_earlier).astype(jnp.bfloat16)
    return dict(
        block_ones=block_ones, query=query, key=key, value=value, factor_query=factor_query,
        factor_key=factor_key, unit_query=unit_query, unit_key=unit_key, key_normed=key_normed,
        forget=forget, key_mix=key_mix, value_mix=value_mix, key_earlier=key_earlier,
        value_earlier=value_earlier, queries=queries, keys=keys, values=values,
    )


def running_sum(values, direction):
    length = values.shape[0]
    rows = row_ids(length)
    step = 1
    while step < length:
        if direction > 0:
            moved = jnp.where(rows >= step, pltpu.roll(values, step, 0), 0.0)
        else:
            moved = jnp.where(rows < length - step, pltpu.roll(values, length - step, 0), 0.0)
        values = values + moved
        step *= 2
    return values


def masked_head(values, head):
    lane = lane_ids(values.shape[0])
    keep = (lane < LANES // 2) if head == 0 else (lane >= LANES // 2)
    return jnp.where(keep, values, jnp.zeros_like(values))


def causal(scores, width, rows):
    diagonal = scores[:, width - rows :]
    query_index = lax.broadcasted_iota(jnp.int32, (rows, rows), 0)
    key_index = lax.broadcasted_iota(jnp.int32, (rows, rows), 1)
    diagonal = jnp.where(key_index <= query_index, diagonal, -1e30)
    if width == rows:
        return diagonal
    return jnp.concatenate([scores[:, : width - rows], diagonal], axis=1)


def attend_kernel(q_ref, k_ref, v_ref, g_ref, small_ref, bias_ref, gain_ref,
                  gated_ref, attended_ref, shift_ref, heads):
    length = q_ref.shape[0]
    half = LANES // 2
    p = prepare(q_ref, k_ref, v_ref, small_ref, bias_ref, gain_ref, heads)
    x = p["forget"]
    totals = running_sum(jnp.minimum(x, 0.0) - jnp.log1p(jnp.exp(-jnp.abs(x))), 1)
    totals_rows = totals.T
    scaled = p["queries"] * jnp.bfloat16(half ** -0.5)
    rows = min(QROWS, length)
    for start in range(0, length, rows):
        width = start + rows
        outs, shifts = [], []
        for head in range(2):
            query = masked_head(scaled[start:width], head)
            row_total = totals[start:width, head * half : head * half + 1]
            key_total = totals_rows[head * half : head * half + 1, :width]
            scores = dot_abt(query, p["keys"][:width]) + (row_total - key_total)
            exponent = jnp.exp(causal(scores, width, rows))
            row_sum = jnp.sum(exponent, axis=1, keepdims=True)
            probability = (exponent * (1.0 / row_sum)).astype(jnp.bfloat16)
            outs.append(dot_ab(probability, p["values"][:width]))
            shifts.append(row_total - jnp.log(row_sum))
        first = lane_ids(rows) < half
        attended = jnp.where(first, outs[0], outs[1]).astype(jnp.bfloat16)
        shift_ref[start:width, :] = jnp.where(first, shifts[0], shifts[1])
        attended_ref[start:width, :] = attended
        gate = jax.nn.sigmoid(g_ref[start:width, :].astype(jnp.float32))
        gated_ref[start:width, :] = (attended.astype(jnp.float32) * gate).astype(jnp.bfloat16)


def attend_back_kernel(q_ref, k_ref, v_ref, g_ref, small_ref, bias_ref, gain_ref,
                       attended_ref, shift_ref, grad_ref,
                       out_ref, gains_ref, forget_ref,
                       dq_ref, dk_ref, dv_ref, sums_ref, heads):
    length = q_ref.shape[0]
    half = LANES // 2
    pair = pl.program_id(0)
    pairs = heads // 2
    p = prepare(q_ref, k_ref, v_ref, small_ref, bias_ref, gain_ref, heads)
    x = p["forget"]
    totals_rows = running_sum(jnp.minimum(x, 0.0) - jnp.log1p(jnp.exp(-jnp.abs(x))), 1).T
    scale = jnp.bfloat16(half ** -0.5)
    scaled = p["queries"] * scale
    scaled_keys = p["keys"] * scale
    gate = jax.nn.sigmoid(g_ref[...].astype(jnp.float32))
    grad_gated = grad_ref[...].astype(jnp.float32)
    grad_attended = (grad_gated * gate).astype(jnp.bfloat16)

    def put(kind, values):
        at = pl.multiple_of((kind * pairs + pair) * LANES, LANES)
        out_ref[:, pl.ds(at, LANES)] = values.astype(jnp.bfloat16)

    put(3, grad_gated * attended_ref[...].astype(jnp.float32) * gate * (1.0 - gate))
    dk_ref[...] = jnp.zeros_like(dk_ref)
    dv_ref[...] = jnp.zeros_like(dv_ref)
    sums_ref[...] = jnp.zeros_like(sums_ref)
    rows = min(QROWS, length)
    row_parts = []
    for start in range(0, length, rows):
        width = start + rows
        first = lane_ids(rows) < half
        first_wide = lane_ids(width) < half
        dqs, dks, dvs, row_sums = [], [], [], []
        for head in range(2):
            query = masked_head(scaled[start:width], head)
            grad = masked_head(grad_attended[start:width], head)
            key_total = totals_rows[head * half : head * half + 1, :width]
            scores = dot_abt(query, p["keys"][:width]) + (
                shift_ref[start:width, head * half : head * half + 1] - key_total
            )
            probability = jnp.exp(causal(scores, width, rows))
            weighted = probability * dot_abt(grad, p["values"][:width])
            inner = jnp.sum(weighted, axis=1, keepdims=True)
            grad_scores = weighted - probability * inner
            row_sums.append(jnp.sum(grad_scores, axis=1, keepdims=True))
            sums_ref[head : head + 1, :width] += jnp.sum(grad_scores, axis=0, keepdims=True)
            low = grad_scores.astype(jnp.bfloat16)
            dqs.append(dot_ab(low, scaled_keys[:width]))
            dks.append(dot_atb(low, scaled[start:width]))
            dvs.append(dot_atb(probability.astype(jnp.bfloat16), grad_attended[start:width]))
        dq_ref[start:width, :] = jnp.where(first, dqs[0], dqs[1])
        dk_ref[:width, :] += jnp.where(first_wide, dks[0], dks[1])
        dv_ref[:width, :] += jnp.where(first_wide, dvs[0], dvs[1])
        row_parts.append(jnp.where(first, row_sums[0], row_sums[1]))
    lane = lane_ids(length)
    top = lax.broadcasted_iota(jnp.int32, (LANES, length), 0) < half
    columns = jnp.where(top, sums_ref[0:1, :], sums_ref[1:2, :]).T
    grad_totals = jnp.concatenate(row_parts, axis=0) - columns
    grad_forget = running_sum(grad_totals, -1) * (1.0 - jax.nn.sigmoid(x))

    def unshift(grad, mixing, values, earlier):
        carried = mixing * grad
        following = jnp.where(row_ids(length) == length - 1, 0.0, pltpu.roll(carried, length - 1, 0))
        grad_mixing = group_sum(grad * (earlier - values), p["block_ones"])
        return (1.0 - mixing) * grad + following, grad_mixing * mixing * (1.0 - mixing)

    def norm_back(factor, unit, grad):
        inner = group_sum(grad * unit, p["block_ones"]) * (1.0 / half)
        return factor * (grad - unit * inner)

    grad_query = dq_ref[...]
    grad_key, grad_key_mix = unshift(dk_ref[...], p["key_mix"], p["key_normed"], p["key_earlier"])
    grad_value, grad_value_mix = unshift(dv_ref[...], p["value_mix"], p["value"], p["value_earlier"])
    put(0, norm_back(p["factor_query"], p["unit_query"], grad_query * gain_ref[0:1, :]))
    put(1, norm_back(p["factor_key"], p["unit_key"], grad_key * gain_ref[1:2, :]))
    put(2, grad_value)

    @pl.when(pair == 0)
    def _():
        out_ref[:, 4 * pairs * LANES :] = jnp.zeros((length, LANES), jnp.bfloat16)
        gains_ref[...] = jnp.zeros_like(gains_ref)

    gains_ref[0:1, :] += jnp.sum(grad_query * p["unit_query"], axis=0, keepdims=True)
    gains_ref[1:2, :] += jnp.sum(grad_key * p["unit_key"], axis=0, keepdims=True)
    forget_ref[0] = jnp.sum(grad_forget, axis=0, keepdims=True)
    merged = out_ref[:, 4 * pairs * LANES :].astype(jnp.float32)
    for kind, values in enumerate((grad_forget, grad_key_mix, grad_value_mix)):
        swapped = pltpu.roll(values, half, 1)
        first = jnp.where(lane < half, values, swapped)
        second = jnp.where(lane < half, swapped, values)
        column = kind * heads + 2 * pair
        merged = jnp.where(lane == column, first, jnp.where(lane == column + 1, second, merged))
    out_ref[:, 4 * pairs * LANES :] = merged.astype(jnp.bfloat16)


def block_specs(length, pairs):
    def column(kind):
        return pl.BlockSpec((length, LANES), lambda i: (0, kind * pairs + i))

    return [
        column(0), column(1), column(2), column(3),
        pl.BlockSpec((length, LANES), lambda i: (0, 4 * pairs)),
        pl.BlockSpec((1, 1, LANES), lambda i: (i, 0, 0)),
        pl.BlockSpec((2, LANES), lambda i: (0, 0)),
    ]


def attend(projected, bias, gains, heads):
    length = projected.shape[0]
    pairs = heads // 2
    block = pl.BlockSpec((length, LANES), lambda i: (0, i))
    wide = pairs * LANES
    return pl.pallas_call(
        partial(attend_kernel, heads=heads),
        grid=(pairs,),
        in_specs=block_specs(length, pairs),
        out_specs=[block, block, block],
        out_shape=[
            jax.ShapeDtypeStruct((length, wide), jnp.bfloat16),
            jax.ShapeDtypeStruct((length, wide), jnp.bfloat16),
            jax.ShapeDtypeStruct((length, wide), jnp.float32),
        ],
        compiler_params=pltpu.CompilerParams(vmem_limit_bytes=48 * 2**20),
        cost_estimate=pl.CostEstimate(
            flops=2 * 2 * length * length * wide, transcendentals=length * length * heads // 2,
            bytes_accessed=length * wide * 2 * 10,
        ),
        name="attend",
    )(projected, projected, projected, projected, projected, bias, gains)


def attend_back(projected, bias, gains, attended, shift, grad, heads):
    length, full = projected.shape
    pairs = heads // 2
    wide = pairs * LANES
    block = pl.BlockSpec((length, LANES), lambda i: (0, i))
    return pl.pallas_call(
        partial(attend_back_kernel, heads=heads),
        grid=(pairs,),
        in_specs=block_specs(length, pairs) + [block, block, block],
        out_specs=[
            pl.BlockSpec((length, full), lambda i: (0, 0)),
            pl.BlockSpec((2, LANES), lambda i: (0, 0)),
            pl.BlockSpec((1, 1, LANES), lambda i: (i, 0, 0)),
        ],
        out_shape=[
            jax.ShapeDtypeStruct((length, full), jnp.bfloat16),
            jax.ShapeDtypeStruct((2, LANES), jnp.float32),
            jax.ShapeDtypeStruct((pairs, 1, LANES), jnp.float32),
        ],
        scratch_shapes=[
            pltpu.VMEM((length, LANES), jnp.float32),
            pltpu.VMEM((length, LANES), jnp.float32),
            pltpu.VMEM((length, LANES), jnp.float32),
            pltpu.VMEM((8, length), jnp.float32),
        ],
        compiler_params=pltpu.CompilerParams(vmem_limit_bytes=48 * 2**20),
        cost_estimate=pl.CostEstimate(
            flops=5 * 2 * length * length * wide, transcendentals=length * length * heads // 2,
            bytes_accessed=length * wide * 2 * 16,
        ),
        name="attend_back",
    )(projected, projected, projected, projected, projected, bias, gains, attended, shift, grad)


def inverse_norm(values):
    return lax.rsqrt(jnp.mean(values * values, axis=-1, keepdims=True) + epsilon)


def norm_back(values, factor, grad_normed):
    normed = values * factor
    inner_mean = jnp.mean(grad_normed * normed, axis=-1, keepdims=True)
    return factor * (grad_normed - normed * inner_mean)


def swap_with(values, axis, bit):
    size = lax.axis_size(axis)
    return lax.ppermute(values, axis, [(i, i ^ bit) for i in range(size)])


def line_gather(block, axis):
    size = lax.axis_size(axis)
    index = lax.axis_index(axis)
    rows = block.shape[0]
    rising, falling = [], []
    up = down = block
    for _ in range(size - 1):
        up = lax.ppermute(up, axis, [(i, i + 1) for i in range(size - 1)])
        down = lax.ppermute(down, axis, [(i + 1, i) for i in range(size - 1)])
        rising.append(up)
        falling.append(down)
    ordered = jnp.concatenate(rising[::-1] + [block] + falling, axis=0)
    return lax.dynamic_slice_in_dim(ordered, (size - 1 - index) * rows, size * rows, 0)


def line_scatter(partial_rows, axis):
    size = lax.axis_size(axis)
    index = lax.axis_index(axis)
    rows = partial_rows.shape[0] // size

    def part(at):
        return lax.dynamic_slice_in_dim(partial_rows, jnp.clip(at, 0, size - 1) * rows, rows, 0)

    up = down = None
    for step in range(1, size):
        far = size - step
        above, below = part(index + far), part(index - far)
        if up is not None:
            above, below = above + up, below + down
        up = lax.ppermute(
            above.astype(jnp.bfloat16), axis, [(i, i + 1) for i in range(size - 1)]
        ).astype(jnp.float32)
        down = lax.ppermute(
            below.astype(jnp.bfloat16), axis, [(i + 1, i) for i in range(size - 1)]
        ).astype(jnp.float32)
    return part(index) + up + down


def sum_everywhere(values, axes):
    for axis in axes:
        bit = 1
        while bit < lax.axis_size(axis):
            values = values + swap_with(values, axis, bit)
            bit *= 2
    return values


def body(
    inputs,
    norm_attn,
    w_proj,
    w_small,
    forget_bias,
    qk_gain,
    w_out,
    norm_ffn,
    w_in,
    w_down,
    cotangent,
):
    row_count, model_width = inputs.shape
    weight_rows = w_proj.shape[0]
    seq_parts = lax.axis_size("seq")
    fsdp_parts = lax.axis_size("fsdp")
    seq_at = lax.axis_index("seq")
    side = seq_at % 2
    head_count = forget_bias.shape[0]
    head_width = qk_gain.shape[1]
    heads = head_count // seq_parts
    wide = heads * head_width
    small_wide = 3 * heads
    length = row_count * seq_parts
    hidden_rows = w_down.shape[0]
    hidden_half = fsdp_parts * hidden_rows // 2

    every_input = line_gather(inputs, "seq")
    local_proj = lax.dynamic_index_in_dim(
        w_proj.reshape(weight_rows, 4, seq_parts, wide), seq_at, 2, False
    ).reshape(weight_rows, 4 * wide)
    local_small = lax.dynamic_index_in_dim(
        w_small.reshape(weight_rows, 3, seq_parts, heads), seq_at, 2, False
    ).reshape(weight_rows, small_wide)
    packed = jnp.concatenate(
        [
            local_proj,
            local_small,
            norm_attn[:, None],
            norm_ffn[:, None],
            jnp.zeros((weight_rows, LANES - small_wide - 2), jnp.bfloat16),
        ],
        axis=1,
    )
    packed_full = lax.all_gather(packed, "fsdp", axis=0, tiled=True)
    gain_attention = packed_full[:, 4 * wide + small_wide].astype(jnp.float32)
    gain_ffn = packed_full[:, 4 * wide + small_wide + 1].astype(jnp.float32)
    out_full = lax.all_gather(w_out, "fsdp", axis=0, tiled=True)
    in_half = lax.dynamic_index_in_dim(
        w_in.reshape(weight_rows, 2, fsdp_parts, 2, hidden_rows // 2), side, 3, False
    ).reshape(weight_rows, 2 * hidden_half)
    in_half = lax.all_gather(in_half, "fsdp", axis=0, tiled=True)
    down_half = lax.dynamic_index_in_dim(
        w_down.reshape(2, hidden_rows // 2, model_width), side, 0, False
    )
    down_half = lax.all_gather(down_half, "fsdp", axis=0, tiled=True)
    cotangent_pair = jnp.concatenate([cotangent, swap_with(cotangent, "seq", 1)], axis=0)

    wide_input = every_input.astype(jnp.float32)
    normed = (wide_input * inverse_norm(wide_input) * gain_attention).astype(jnp.bfloat16)
    projected = dot_ab(normed, packed_full).astype(jnp.bfloat16)
    bias_lanes = jnp.repeat(
        lax.dynamic_slice_in_dim(forget_bias, seq_at * heads, heads, 0), head_width
    ).reshape(heads // 2, 1, LANES)
    gain_lanes = jnp.tile(qk_gain.astype(jnp.float32), (1, 2))
    gated, attended, shift = attend(projected, bias_lanes, gain_lanes, heads)
    mixed_rows = lax.all_to_all(gated, "seq", split_axis=0, concat_axis=1, tiled=True)

    source = inputs.astype(jnp.float32)
    residual = source + dot_ab(mixed_rows, out_full)
    factor_ffn = inverse_norm(residual)
    unit_ffn = residual * factor_ffn
    normed_ffn = (unit_ffn * gain_ffn).astype(jnp.bfloat16)
    normed_pair = jnp.concatenate([normed_ffn, swap_with(normed_ffn, "seq", 1)], axis=0)
    gate_up = dot_ab(normed_pair, in_half)
    gate_part = gate_up[:, :hidden_half]
    up_part = gate_up[:, hidden_half:]
    inner_sigmoid = jax.nn.sigmoid(gate_part)
    silu_gate = gate_part * inner_sigmoid
    activated = (silu_gate * up_part).astype(jnp.bfloat16)
    down_part = dot_ab(activated, down_half)
    output = (
        residual
        + down_part[:row_count]
        + swap_with(down_part[row_count:].astype(jnp.bfloat16), "seq", 1).astype(jnp.float32)
    ).astype(jnp.bfloat16)

    grad_act = dot_abt(cotangent_pair, down_half)
    grad_gate = grad_act * up_part * inner_sigmoid * (1.0 + gate_part * (1.0 - inner_sigmoid))
    grad_up = grad_act * silu_gate
    grad_gate_up = jnp.concatenate([grad_gate, grad_up], axis=1).astype(jnp.bfloat16)
    back_part = dot_abt(grad_gate_up, in_half)
    grad_normed_ffn = back_part[:row_count] + swap_with(
        back_part[row_count:].astype(jnp.bfloat16), "seq", 1
    ).astype(jnp.float32)
    grad_residual = cotangent.astype(jnp.float32) + norm_back(
        residual, factor_ffn, grad_normed_ffn * gain_ffn
    )
    grad_branch = grad_residual.astype(jnp.bfloat16)
    grad_mixed = dot_abt(grad_branch, out_full).astype(jnp.bfloat16)
    grad_heads = lax.all_to_all(grad_mixed, "seq", split_axis=1, concat_axis=0, tiled=True)
    grad_down = dot_atb(activated, cotangent_pair).astype(jnp.bfloat16)
    grad_in = dot_atb(normed_pair, grad_gate_up).astype(jnp.bfloat16)
    grad_out = dot_atb(mixed_rows, grad_branch).astype(jnp.bfloat16)
    grad_in = lax.psum_scatter(grad_in, "fsdp", scatter_dimension=0, tiled=True)
    grad_down = lax.psum_scatter(grad_down, "fsdp", scatter_dimension=0, tiled=True)
    grad_out = lax.psum_scatter(grad_out, "fsdp", scatter_dimension=0, tiled=True)

    grad_projected, gain_sums, forget_sums = attend_back(
        projected, bias_lanes, gain_lanes, attended, shift, grad_heads, heads
    )
    grad_packed = dot_atb(normed, grad_projected).astype(jnp.bfloat16)
    grad_packed = lax.psum_scatter(grad_packed, "fsdp", scatter_dimension=0, tiled=True)
    grad_normed = line_scatter(dot_abt(grad_projected, packed_full), "seq")
    grad_inputs = grad_residual + norm_back(
        source, inverse_norm(source), grad_normed * gain_attention
    )

    bias_row = lax.dynamic_update_slice_in_dim(
        jnp.zeros((LANES,), jnp.float32),
        forget_sums.reshape(heads, head_width)[:, 0],
        seq_at * heads,
        0,
    )
    sums = sum_everywhere(jnp.concatenate([gain_sums, bias_row[None]], axis=0), ("fsdp", "seq"))
    grad_qk_gain = sums[:2, :head_width] + sums[:2, head_width:]
    grad_forget_bias = sums[2, :head_count]

    def whole_hidden(half):
        total = half.astype(jnp.float32)
        bit = 2
        while bit < seq_parts:
            moved = swap_with(total.astype(jnp.bfloat16), "seq", bit).astype(jnp.float32)
            total = total + moved
            bit *= 2
        total = total.astype(jnp.bfloat16)
        other = swap_with(total, "seq", 1)
        first = jnp.where(side == 0, total, other)
        second = jnp.where(side == 0, other, total)
        return first.astype(jnp.float32), second.astype(jnp.float32)

    first, second = whole_hidden(grad_in)
    folded = (weight_rows, 2, fsdp_parts, 1, hidden_rows // 2)
    grad_in = jnp.concatenate([first.reshape(folded), second.reshape(folded)], axis=3).reshape(
        weight_rows, 4 * hidden_half
    )
    grad_down = jnp.concatenate(whole_hidden(grad_down), axis=0)
    grad_out = lax.psum(grad_out, "seq").astype(jnp.float32)
    every_packed = lax.all_gather(grad_packed, "seq", axis=0, tiled=False).astype(jnp.float32)
    grad_proj = jnp.moveaxis(
        every_packed[:, :, : 4 * wide].reshape(seq_parts, weight_rows, 4, wide), 0, 2
    ).reshape(weight_rows, 4 * seq_parts * wide)
    grad_small = jnp.moveaxis(
        every_packed[:, :, 4 * wide : 4 * wide + small_wide].reshape(
            seq_parts, weight_rows, 3, heads
        ),
        0,
        2,
    ).reshape(weight_rows, 3 * head_count)
    grad_gain_attention = (
        jnp.sum(grad_proj * w_proj.astype(jnp.float32), axis=1)
        + jnp.sum(grad_small * w_small.astype(jnp.float32), axis=1)
    ) / norm_attn.astype(jnp.float32)
    grad_gain_ffn = jnp.sum(grad_in * w_in.astype(jnp.float32), axis=1) / norm_ffn.astype(
        jnp.float32
    )
    return (
        output,
        grad_inputs,
        grad_gain_attention,
        grad_proj,
        grad_small,
        grad_forget_bias,
        grad_qk_gain,
        grad_out,
        grad_gain_ffn,
        grad_in,
        grad_down,
    )


def solution(mesh):
    in_specs = (
        P(("fsdp", "seq"), None),
        P("fsdp"),
        P("fsdp", None),
        P("fsdp", None),
        P(),
        P(),
        P("fsdp", None),
        P("fsdp"),
        P("fsdp", None),
        P("fsdp", None),
        P(("fsdp", "seq"), None),
    )
    out_specs = (
        P(("fsdp", "seq"), None),
        P(("fsdp", "seq"), None),
        P("fsdp"),
        P("fsdp", None),
        P("fsdp", None),
        P(),
        P(),
        P("fsdp", None),
        P("fsdp"),
        P("fsdp", None),
        P("fsdp", None),
    )
    return jax.shard_map(body, mesh=mesh, in_specs=in_specs, out_specs=out_specs, check_vma=False)
```

time: 1400 us -> 797 us (0.57)
  waiting for transfers between devices: 620 us -> 404 us
  blocking collectives: 186 us -> 24.2 us
  matrix products: 239 us -> 103 us
  local copies, waits for them, and re-layouts: 188 us -> 96.8 us
  Pallas kernels: 0 us -> 45.9 us
  loops' own time: 45.7 us -> 0 us
  starting transfers between devices: 18.8 us -> 61.5 us
  other arithmetic: 72.2 us -> 39.4 us
    ppermute x0 -> x25, waiting for transfers between devices: none -> 185 us  [the longest x13 109 us: swap_with(): return lax.ppermute(values, axis, [(i, i ^ bit) for i in range(size)])]
    reduce_scatter x4, waiting for transfers between devices: 248 us -> 89.4 us  [the longest x1 60.9 us: body(): lax.psum_scatter(grad_down, 'fsdp', scatter_dimension=0, tiled=True)]
    psum x1, waiting for transfers between devices: 202 us -> 52.7 us  [body(): grad_out = lax.psum(grad_out, 'seq').astype(jnp.float32)]
    dot_general x99 -> x12, matrix products: 239 us -> 103 us  [the longest x4 37.4 us: dot_abt(): lax.dot_general(a, b, (((1,), (1,)), ((), ())), preferred_element_type=jn...]
    all_to_all x4 -> x1, waiting for transfers between devices: 97.7 us -> 14.7 us  [body(): lax.all_to_all(gated, 'seq', split_axis=0, concat_axis=1, tiled=True)]
    psum x2 -> x0, blocking collectives: 65.1 us -> none  [the longest x1 39.3 us: body(): lax.psum((grad_norm_gains, grad_bias), ('fsdp', 'seq'))]
    all_to_all x2 -> x1, blocking collectives: 82 us -> 24.2 us  [body(): lax.all_to_all(grad_mixed, 'seq', split_axis=1, concat_axis=0, tiled=True)]
    ppermute x0 -> x25, starting transfers between devices: none -> 56.6 us  [the longest x13 23.3 us: swap_with(): return lax.ppermute(values, axis, [(i, i ^ bit) for i in range(size)])]
  transfers between devices with their start and end apart: 14 -> 36, of which waited for: 7 -> 22; matrix products, arithmetic and copies ran while one was open for 32% -> 21% of each run, Pallas kernels for 0% -> 6%
where the time goes in v1:
time: 797 us; the launch traced here: 790 us
  waiting for transfers between devices  404 us (51%)
  matrix products  103 us (13%)
  local copies, waits for them, and re-layouts  96.8 us (12%)
  starting transfers between devices  61.5 us (8%)
  Pallas kernels  45.9 us (6%)
  other arithmetic  39.4 us (5%)
  blocking collectives  24.2 us (3%)
  between operations  15.1 us (2%)
    ppermute x13, waiting for transfers between devices, swap_with(): return lax.ppermute(values, axis, [(i, i ^ bit) for i in range(size)])  109 us
    reduce_scatter x1, waiting for transfers between devices, body(): lax.psum_scatter(grad_down, 'fsdp', scatter_dimension=0, tiled=True)  60.9 us
    psum x1, waiting for transfers between devices, body(): grad_out = lax.psum(grad_out, 'seq').astype(jnp.float32)  52.7 us
    ppermute x3, waiting for transfers between devices, line_gather(): up = lax.ppermute(up, axis, [(i, i + 1) for i in range(size - 1)])  41.6 us
    all_gather x1, waiting for transfers between devices, body(): lax.all_gather(grad_packed, 'seq', axis=0, tiled=False).astype(jnp.float32)  40 us
    dot_general x4, matrix products, dot_abt(): lax.dot_general(a, b, (((1,), (1,)), ((), ())), preferred_element_type=jn...  37.4 us
    dot_general x4, matrix products, dot_ab(): lax.dot_general(a, b, (((1,), (0,)), ((), ())), preferred_element_type=jn...  33 us
    dot_general x4, matrix products, dot_atb(): lax.dot_general(a, b, (((0,), (0,)), ((), ())), preferred_element_type=jn...  32.6 us
  transfers between devices with their start and end apart: 36, of which 22 were waited for; matrix products, arithmetic and copies ran while one was open for 21% of the time, Pallas kernels for 6%

profile of v1, /device:TPU:0, one launch (start us, length us, event | category | flops | bytes accessed | tf_op | source)
XLA Modules:
  0.0 789.9 jit_solution(13252535466942211329)
XLA Ops:
  7.3 4.8 reshape.141
  12.0 5.4 dynamic-slice_reduce_fusion.1
  20.3 6.1 reshape.145
  26.4 12.6 %dynamic-slice_reduce_fusion = bf16[192,2,8,256]{3,2,1,0:T(8,128)(2,1)} fusion(bf16[192,2,8,2,256]{4,3,2,1,0:T(2,128)(2,1)} %reshape.145, s32[]{:T(128)S(6)} %select_n.77), kind=kLoop, calls=%fused_computation.25 | loop fusion | bytes 3145732 | tf_op jit(solution)/shard_map/jit(dynamic_index_in_dim)/dynamic_slice | solution.py:418
  43.3 5.2 collective-permute-start
  49.8 15.4 %collective-permute-done = bf16[256,1536]{1,0:T(8,128)(2,1)S(1)} collective-permute-done((bf16[256,1536]{1,0:T(8,128)(2,1)S(1)}, bf16[256,1536]{1,0:T(8,128)(2,1)S(1)}, u32[]{:S(2)}, u32[]{:S(2)}) %collective-permute-start) | collective-permute-done | bytes 786464 | tf_op jit(solution)/shard_map/ppermute | solution.py:329
  65.2 5.3 collective-permute-start.1
  71.8 13.7 %collective-permute-done.1 = bf16[256,1536]{1,0:T(8,128)(2,1)} collective-permute-done((bf16[256,1536]{1,0:T(8,128)(2,1)S(1)}, bf16[256,1536]{1,0:T(8,128)(2,1)}, u32[]{:S(2)}, u32[]{:S(2)}) %collective-permute-start.1) | collective-permute-done | bytes 786464 | tf_op jit(solution)/shard_map/ppermute | solution.py:329
  85.5 5.4 collective-permute-start.2
  92.7 12.5 %collective-permute-done.2 = bf16[256,1536]{1,0:T(8,128)(2,1)} collective-permute-done((bf16[256,1536]{1,0:T(8,128)(2,1)}, bf16[256,1536]{1,0:T(8,128)(2,1)}, u32[]{:S(2)}, u32[]{:S(2)}) %collective-permute-start.2) | collective-permute-done | bytes 786464 | tf_op jit(solution)/shard_map/ppermute | solution.py:329
  115.5 10.7 %convolution_convert_fusion.4.q_ref.k_ref.v_ref.g_ref.small_ref = bf16[1024,1664]{1,0:T(8,128)(2,1)} fusion(bf16[1536,1664]{1,0:T(8,128)(2,1)} %all-gather.8.cloned.1.call-done, f32[1536]{0:T(1024)S(1)} %get-tuple-element.24, f32[1024]{0:T(1024)S(1)} %add_rsqrt_fusion, bf16[1792,1536]{1,0:T(8,128)(2,1)} %copy-done.11, s32[]{:T(128)S(6)} %select_n.73), kind=kOutput, calls=%fused_computation.22 | convolution fusion | flops 5242486784 | bytes 11675652 | tf_op jit(solution)/shard_map/dot_general | solution.py:16
  126.2 15.6 %attend.1 = (bf16[1024,384]{1,0:T(8,128)(2,1)S(1)}, bf16[1024,384]{1,0:T(8,128)(2,1)S(1)}, f32[1024,384]{1,0:T(8,128)S(1)}) custom-call(bf16[1024,1664]{1,0:T(8,128)(2,1)} %convolution_convert_fusion.4.q_ref.k_ref.v_ref.g_ref.small_ref, bf16[1024,1664]{1,0:T(8,128)(2,1)} %convolution_convert_fusion.4.q_ref.k_ref.v_ref.g_ref.small_ref, ...), custom_call_target="tpu_custom_call" | custom-call | flops 1610612736 | bytes 7864320 | tf_op jit(solution)/shard_map/attend/pallas_call | solution.py:254
  149.0 14.7 %all-to-all-done = bf16[4,256,384]{1,2,0:T(8,128)(2,1)S(1)} async-done(((bf16[4,256,384]{1,2,0:T(8,128)(2,1)}), bf16[4,256,384]{1,2,0:T(8,128)(2,1)S(1)}, u32[]{:S(2)}, u32[]{:S(2)}) %all-to-all-start) | async-done | bytes 786464 | tf_op jit(solution)/shard_map/all_to_all | solution.py:436
  163.7 4.1 multiply_reduce_fusion.3
  172.0 6.1 collective-permute-done.8
  180.2 12.8 %collective-permute-done.6 = bf16[256,1536]{1,0:T(8,128)(2,1)} collective-permute-done((bf16[256,1536]{1,0:T(8,128)(2,1)S(1)}, bf16[256,1536]{1,0:T(8,128)(2,1)}, u32[]{:S(2)}, u32[]{:S(2)}) %collective-permute-start.6) | collective-permute-done | bytes 786464 | tf_op jit(solution)/shard_map/ppermute | solution.py:319
  193.0 12.0 %fusion.19 = f32[512,4096]{1,0:T(8,128)} fusion(bf16[1536,4096]{1,0:T(8,128)(2,1)} %all-gather.12.cloned.1.call-done, bf16[256,1536]{1,0:T(8,128)(2,1)} %collective-permute-done.6, bf16[256,1536]{1,0:T(8,128)(2,1)} %copy-done.13), kind=kOutput, calls=%fused_computation.62 | convolution fusion | flops 6445596672 | bytes 22544384 | tf_op jit(solution)/shard_map/dot_general | solution.py:16
  205.0 20.7 %all-gather.14.cloned.1.call-done = bf16[1,2048,1536]{2,1,0:T(8,128)(2,1)} async-done(((bf16[1,256,1536]{2,1,0:T(8,128)(2,1)}), bf16[1,2048,1536]{2,1,0:T(8,128)(2,1)}) %all-gather.14.cloned.1.call-update) | async-done | bytes 6291472 | tf_op jit(solution)/shard_map/all_gather | solution.py:425
  225.8 10.4 %multiply_convert_fusion.1 = (bf16[512,2048]{1,0:T(8,128)(2,1)S(1)}, bf16[512,2048]{1,0:T(8,128)(2,1)S(1)}, bf16[512,2048]{1,0:T(8,128)(2,1)S(1)}) fusion(f32[512,4096]{1,0:T(8,128)} %fusion.19, bf16[512,1536]{1,0:T(8,128)(2,1)} %constant_dynamic-update-slice_fusion.7, bf16[1,2048,1536]{2,1,0:T(8,128)(2,1)} %all-gather.14.cloned.1.call-done), kind=kOutput, calls=%fused_computation.18 | convolution fusion | flops 3236954112 | bytes 22544384 | tf_op jit(solution)/shard_map/dot_general | solution.py:20
  236.2 12.1 %fusion.8 = f32[512,1536]{1,0:T(8,128)S(1)} fusion(bf16[1536,4096]{1,0:T(8,128)(2,1)} %all-gather.12.cloned.1.call-done, bf16[512,2048]{1,0:T(8,128)(2,1)S(1)} %get-tuple-element.26, bf16[512,2048]{1,0:T(8,128)(2,1)S(1)} %get-tuple-element.25), kind=kOutput, calls=%fused_computation.27 | convolution fusion | flops 6450839552 | bytes 19922944 | tf_op jit(solution)/shard_map/dot_general | solution.py:20
  250.0 6.1 fusion.5
  256.9 12.0 %collective-permute-done.9 = bf16[256,1536]{1,0:T(8,128)(2,1)S(1)} collective-permute-done((bf16[256,1536]{1,0:T(8,128)(2,1)S(1)}, bf16[256,1536]{1,0:T(8,128)(2,1)S(1)}, u32[]{:S(2)}, u32[]{:S(2)}) %collective-permute-start.9) | collective-permute-done | bytes 786464 | tf_op jit(solution)/shard_map/ppermute | solution.py:319
  269.4 15.7 %collective-permute-done.7 = bf16[256,1536]{1,0:T(8,128)(2,1)S(1)} collective-permute-done((bf16[256,1536]{1,0:T(8,128)(2,1)S(1)}, bf16[256,1536]{1,0:T(8,128)(2,1)S(1)}, u32[]{:S(2)}, u32[]{:S(2)}) %collective-permute-start.7) | collective-permute-done | bytes 786464 | tf_op jit(solution)/shard_map/ppermute | solution.py:319
  291.6 4.4 convolution_convert_fusion.5
  296.0 24.2 %all_to_all.38 = bf16[256,4,384]{2,0,1:T(8,128)(2,1)S(1)} all-to-all(bf16[256,4,384]{2,0,1:T(8,128)(2,1)S(1)} %bitcast.78), channel_id=1, replica_groups=mesh['fsdp'=8,'seq'=4] {'seq'}, dimensions={1} | all-to-all | bytes 1572864 | tf_op jit(solution)/shard_map/all_to_all | solution.py:470
  320.2 30.2 %attend_back.1 = (bf16[1024,1664]{1,0:T(8,128)(2,1)}, f32[2,128]{1,0:T(2,128)S(1)}, f32[3,1,128]{2,1,0:T(1,128)S(1)}) custom-call(bf16[1024,1664]{1,0:T(8,128)(2,1)} %convolution_convert_fusion.4.q_ref.k_ref.v_ref.g_ref.small_ref, bf16[1024,1664]{1,0:T(8,128)(2,1)} %convolution_convert_fusion.4.q_ref.k_ref.v_ref.g_ref.small_ref, ...), custom_call_target="tpu_custom_call" | custom-call | flops 4026531840 | bytes 12582912 | tf_op jit(solution)/shard_map/attend_back/pallas_call | solution.py:278
  350.5 10.1 %convolution_convert_fusion.1 = bf16[1536,1664]{1,0:T(8,128)(2,1)} fusion(bf16[1024,1664]{1,0:T(8,128)(2,1)} %get-tuple-element.20, f32[1536]{0:T(1024)S(1)} %get-tuple-element.24, f32[1024]{0:T(1024)S(1)} %add_rsqrt_fusion, bf16[1792,1536]{1,0:T(8,128)(2,1)S(1)} %bitcast.80, s32[]{:T(128)S(6)} %select_n.73), kind=kOutput, calls=%fused_computation.3 | convolution fusion | flops 5243338752 | bytes 11677700 | tf_op jit(solution)/shard_map/dot_general | solution.py:24
  361.7 12.0 %convolution_convert_fusion = bf16[1536,4096]{1,0:T(8,128)(2,1)} fusion(bf16[512,2048]{1,0:T(8,128)(2,1)} %copy-done.27, bf16[512,2048]{1,0:T(8,128)(2,1)} %copy-done.26, bf16[256,1536]{1,0:T(8,128)(2,1)} %collective-permute-done.6, bf16[256,1536]{1,0:T(8,128)(2,1)S(1)} %copy-done.14), kind=kOutput, calls=%fused_computation | convolution fusion | flops 6460276736 | bytes 18350080 | tf_op jit(solution)/shard_map/dot_general | solution.py:24
  375.3 6.9 convolution_convert_fusion.2
  382.3 10.5 %fusion.30 = f32[1024,1536]{1,0:T(8,128)} fusion(bf16[1024,1664]{1,0:T(8,128)(2,1)} %get-tuple-element.20, bf16[1536,1664]{1,0:T(8,128)(2,1)} %all-gather.8.cloned.1.call-done), kind=kOutput, calls=%fused_computation.98 | convolution fusion | flops 5234491392 | bytes 14811136 | tf_op jit(solution)/shard_map/dot_general | solution.py:20
  399.2 14.2 %collective-permute-done.10 = bf16[256,1536]{1,0:T(8,128)(2,1)S(1)} collective-permute-done((bf16[256,1536]{1,0:T(8,128)(2,1)S(1)}, bf16[256,1536]{1,0:T(8,128)(2,1)S(1)}, u32[]{:S(2)}, u32[]{:S(2)}) %collective-permute-start.10) | collective-permute-done | bytes 786464 | tf_op jit(solution)/shard_map/ppermute | solution.py:351
  415.0 4.4 collective-permute-start.11
  419.4 14.7 %collective-permute-done.11 = bf16[256,1536]{1,0:T(8,128)(2,1)S(1)} collective-permute-done((bf16[256,1536]{1,0:T(8,128)(2,1)S(1)}, bf16[256,1536]{1,0:T(8,128)(2,1)S(1)}, u32[]{:S(2)}, u32[]{:S(2)}) %collective-permute-start.11) | collective-permute-done | bytes 786464 | tf_op jit(solution)/shard_map/ppermute | solution.py:351
  434.1 4.0 add_convert_fusion.4
  461.3 5.2 collective-permute-start.20
  466.5 14.7 %collective-permute-done.20 = f32[3,128]{1,0:T(4,128)S(1)} collective-permute-done((f32[3,128]{1,0:T(4,128)S(1)}, f32[3,128]{1,0:T(4,128)S(1)}, u32[]{:S(2)}, u32[]{:S(2)}) %collective-permute-start.20) | collective-permute-done | bytes 1568 | tf_op jit(solution)/shard_map/ppermute | solution.py:319
  482.3 28.5 %reduce-scatter.9.cloned.1.call-done = bf16[192,4096]{1,0:T(8,128)(2,1)} async-done(((bf16[1536,4096]{1,0:T(8,128)(2,1)}), bf16[192,4096]{1,0:T(8,128)(2,1)}) %reduce-scatter.9.cloned.1.call-update) | async-done | bytes 1572880 | tf_op jit(solution)/shard_map/reduce_scatter | solution.py:474
  515.5 60.9 %reduce-scatter.11.cloned.1.call-done = bf16[256,1536]{1,0:T(8,128)(2,1)} async-done(((bf16[2048,1536]{1,0:T(8,128)(2,1)}), bf16[256,1536]{1,0:T(8,128)(2,1)}) %reduce-scatter.11.cloned.1.call-update) | async-done | bytes 786448 | tf_op jit(solution)/shard_map/reduce_scatter | solution.py:475
  582.2 52.7 %all-reduce.2.cloned.1.call-done = bf16[192,1536]{1,0:T(8,128)(2,1)} async-done(((bf16[192,1536]{1,0:T(8,128)(2,1)}), bf16[192,1536]{1,0:T(8,128)(2,1)}) %all-reduce.2.cloned.1.call-update) | async-done | bytes 589840 | tf_op jit(solution)/shard_map/psum | solution.py:517
  643.9 41.0 %collective-permute-done.24 = bf16[256,1536]{1,0:T(8,128)(2,1)S(1)} collective-permute-done((bf16[256,1536]{1,0:T(8,128)(2,1)S(1)}, bf16[256,1536]{1,0:T(8,128)(2,1)S(1)}, u32[]{:S(2)}, u32[]{:S(2)}) %collective-permute-start.24) | collective-permute-done | bytes 786464 | tf_op jit(solution)/shard_map/ppermute | solution.py:319
  687.1 40.0 %all-gather.16.cloned.1.call-done = bf16[768,1664]{1,0:T(8,128)(2,1)} async-done(((bf16[192,1664]{1,0:T(8,128)(2,1)}), bf16[768,1664]{1,0:T(8,128)(2,1)}) %all-gather.16.cloned.1.call-update) | async-done | bytes 2555920 | tf_op jit(solution)/shard_map/all_gather | solution.py:518
  727.1 4.5 slice.66
  732.6 6.2 reshape.148
  738.7 7.5 copy.63
  746.2 6.4 reshape.149
  759.8 8.9 %copy.51 = f32[192,2,8,2,256]{4,3,2,1,0:T(2,128)} copy(f32[192,2,8,2,256]{4,2,1,0,3:T(8,128)S(1)} %maximum_convert_fusion) | data formatting | bytes 12582912 | tf_op jit(solution)/shard_map/reshape | solution.py:513
  768.7 9.1 %reshape.160 = f32[192,8192]{1,0:T(8,128)} reshape(f32[192,2,8,2,256]{4,3,2,1,0:T(2,128)} %copy.51) | data formatting | bytes 12582912 | tf_op jit(solution)/shard_map/reshape | solution.py:513
  777.8 4.4 multiply_reduce_fusion
  (198 shorter events, 109.7 us)
Async XLA Ops:
  7.2 35.2 %copy-start = (bf16[512,1536]{1,0:T(8,128)(2,1)S(1)}, bf16[512,1536]{1,0:T(8,128)(2,1)}, u32[]{:S(2)}) copy-start(bf16[512,1536]{1,0:T(8,128)(2,1)} %param.20) | copy-start | bytes 4718596
  7.2 106.5 %all-gather.8.cloned.1.call-start = ((), (), s32[]{:S(2)}) async-start(), calls=%async_computation.6 | async-start | bytes 5750784 | tf_op jit(solution)/shard_map/all_gather | solution.py:414
  19.0 129.9 %all-gather.10.cloned.1.call-start = ((), (), s32[]{:S(2)}) async-start(), calls=%async_computation.7 | async-start | bytes 5308416 | tf_op jit(solution)/shard_map/all_gather | solution.py:417
  19.8 173.2 %all-gather.12.cloned.1.call-start = ((), (), s32[]{:S(2)}) async-start(), calls=%async_computation.8 | async-start | bytes 14155776 | tf_op jit(solution)/shard_map/all_gather | solution.py:421
  39.0 51.9 %copy-start.23 = (f32[24]{0:T(128)S(1)}, f32[24]{0:T(128)}, u32[]{:S(2)}) copy-start(f32[24]{0:T(128)} %param.15) | copy-start | bytes 292
  39.0 52.2 %copy-start.22 = (bf16[2,64]{1,0:T(2,128)(2,1)S(1)}, bf16[2,64]{1,0:T(2,128)(2,1)}, u32[]{:S(2)}) copy-start(bf16[2,64]{1,0:T(2,128)(2,1)} %param.16) | copy-start | bytes 772
  42.3 183.5 %all-gather.14.cloned.1.call-start = ((), (), s32[]{:S(2)}) async-start(), calls=%async_computation.14 | async-start | bytes 7077888 | tf_op jit(solution)/shard_map/all_gather | solution.py:425
  43.3 21.9 %collective-permute-start = (bf16[256,1536]{1,0:T(8,128)(2,1)S(1)}, bf16[256,1536]{1,0:T(8,128)(2,1)S(1)}, u32[]{:S(2)}, u32[]{:S(2)}) collective-permute-start(bf16[256,1536]{1,0:T(8,128)(2,1)S(1)} %copy-done.4), channel_id=1, source_target_pairs={{0,1},{1,2},{2,3},{4,5},{5,6},{6,7},{8,9},{9,10},{10,11},{12,13},{... | collective-permute-start | bytes 2359304 | tf_op jit(solution)/shard_map/ppermute | solution.py:329
  48.5 22.0 %collective-permute-start.3 = (bf16[256,1536]{1,0:T(8,128)(2,1)S(1)}, bf16[256,1536]{1,0:T(8,128)(2,1)S(1)}, u32[]{:S(2)}, u32[]{:S(2)}) collective-permute-start(bf16[256,1536]{1,0:T(8,128)(2,1)S(1)} %copy-done.4), channel_id=1, source_target_pairs={{1,0},{2,1},{3,2},{5,4},{6,5},{7,6},{9,8},{10,9},{11,10},{13,12},{... | collective-permute-start | bytes 2359304 | tf_op jit(solution)/shard_map/ppermute | solution.py:330
  65.2 20.2 %collective-permute-start.1 = (bf16[256,1536]{1,0:T(8,128)(2,1)S(1)}, bf16[256,1536]{1,0:T(8,128)(2,1)}, u32[]{:S(2)}, u32[]{:S(2)}) collective-permute-start(bf16[256,1536]{1,0:T(8,128)(2,1)S(1)} %collective-permute-done), channel_id=1, source_target_pairs={{0,1},{1,2},{2,3},{4,5},{5,6},{6,7},{8,9},{9,10},{10,11},{12,13},{... | collective-permute-start | bytes 2359304 | tf_op jit(solution)/shard_map/ppermute | solution.py:329
  70.5 20.8 %collective-permute-start.4 = (bf16[256,1536]{1,0:T(8,128)(2,1)S(1)}, bf16[256,1536]{1,0:T(8,128)(2,1)S(1)}, u32[]{:S(2)}, u32[]{:S(2)}) collective-permute-start(bf16[256,1536]{1,0:T(8,128)(2,1)S(1)} %collective-permute-done.3), channel_id=1, source_target_pairs={{1,0},{2,1},{3,2},{5,4},{6,5},{7,6},{9,8},{10,9},{11,10},{13,12},{... | collective-permute-start | bytes 2359304 | tf_op jit(solution)/shard_map/ppermute | solution.py:330
  85.5 19.7 %collective-permute-start.2 = (bf16[256,1536]{1,0:T(8,128)(2,1)}, bf16[256,1536]{1,0:T(8,128)(2,1)}, u32[]{:S(2)}, u32[]{:S(2)}) collective-permute-start(bf16[256,1536]{1,0:T(8,128)(2,1)} %collective-permute-done.1), channel_id=1, source_target_pairs={{0,1},{1,2},{2,3},{4,5},{5,6},{6,7},{8,9},{9,10},{10,11},{12,13},{... | collective-permute-start | bytes 2359304 | tf_op jit(solution)/shard_map/ppermute | solution.py:329
  91.2 19.2 %collective-permute-start.5 = (bf16[256,1536]{1,0:T(8,128)(2,1)S(1)}, bf16[256,1536]{1,0:T(8,128)(2,1)S(1)}, u32[]{:S(2)}, u32[]{:S(2)}) collective-permute-start(bf16[256,1536]{1,0:T(8,128)(2,1)S(1)} %collective-permute-done.4), channel_id=1, source_target_pairs={{1,0},{2,1},{3,2},{5,4},{6,5},{7,6},{9,8},{10,9},{11,10},{13,12},{... | collective-permute-start | bytes 2359304 | tf_op jit(solution)/shard_map/ppermute | solution.py:330
  143.0 20.7 %all-to-all-start = ((bf16[4,256,384]{1,2,0:T(8,128)(2,1)}), bf16[4,256,384]{1,2,0:T(8,128)(2,1)S(1)}, u32[]{:S(2)}, u32[]{:S(2)}) async-start(bf16[4,256,384]{1,2,0:T(8,128)(2,1)} %copy.44), calls=%async_computation | async-start | bytes 1572864 | tf_op jit(solution)/shard_map/all_to_all | solution.py:436
  146.7 306.6 %reduce-scatter.7.cloned.1.call-start = ((), (), s32[]{:S(2)}) async-start(), calls=%async_computation.10 | async-start | bytes 5308416 | tf_op jit(solution)/shard_map/reduce_scatter | solution.py:476
  146.9 31.3 %collective-permute-start.8 = (bf16[256,1536]{1,0:T(8,128)(2,1)}, bf16[256,1536]{1,0:T(8,128)(2,1)}, u32[]{:S(2)}, u32[]{:S(2)}) collective-permute-start(bf16[256,1536]{1,0:T(8,128)(2,1)} %param.21), channel_id=1, source_target_pairs={{0,1},{1,0},{2,3},{3,2},{4,5},{5,4},{6,7},{7,6},{8,9},{9,8},{10,11... | collective-permute-start | bytes 2359304 | tf_op jit(solution)/shard_map/ppermute | solution.py:319
  169.2 23.8 %collective-permute-start.6 = (bf16[256,1536]{1,0:T(8,128)(2,1)S(1)}, bf16[256,1536]{1,0:T(8,128)(2,1)}, u32[]{:S(2)}, u32[]{:S(2)}) collective-permute-start(bf16[256,1536]{1,0:T(8,128)(2,1)S(1)} %multiply_convert_fusion.3), channel_id=1, source_target_pairs={{0,1},{1,0},{2,3},{3,2},{4,5},{5,4},{6,7},{7,6},{8,9},{9,8},{10,11... | collective-permute-start | bytes 2359304 | tf_op jit(solution)/shard_map/ppermute | solution.py:319
  236.2 13.8 %copy-start.24 = (bf16[512,2048]{1,0:T(8,128)(2,1)}, bf16[512,2048]{1,0:T(8,128)(2,1)S(1)}, u32[]{:S(2)}) copy-start(bf16[512,2048]{1,0:T(8,128)(2,1)S(1)} %get-tuple-element.27) | copy-start | bytes 6291460
  248.5 20.4 %collective-permute-start.9 = (bf16[256,1536]{1,0:T(8,128)(2,1)S(1)}, bf16[256,1536]{1,0:T(8,128)(2,1)S(1)}, u32[]{:S(2)}, u32[]{:S(2)}) collective-permute-start(bf16[256,1536]{1,0:T(8,128)(2,1)S(1)} %slice.95), channel_id=1, source_target_pairs={{0,1},{1,0},{2,3},{3,2},{4,5},{5,4},{6,7},{7,6},{8,9},{9,8},{10,11... | collective-permute-start | bytes 2359304 | tf_op jit(solution)/shard_map/ppermute | solution.py:319
  250.0 18.9 %copy-start.3 = (f32[256,1536]{1,0:T(8,128)S(1)}, f32[256,1536]{1,0:T(8,128)}, u32[]{:S(2)}) copy-start(f32[256,1536]{1,0:T(8,128)} %copy-done.2) | copy-start | bytes 4718596
  256.1 28.9 %copy-start.10 = (bf16[256,1536]{1,0:T(8,128)(2,1)S(1)}, bf16[256,1536]{1,0:T(8,128)(2,1)}, u32[]{:S(2)}) copy-start(bf16[256,1536]{1,0:T(8,128)(2,1)} %param.21) | copy-start | bytes 2359300
  256.2 28.8 %collective-permute-start.7 = (bf16[256,1536]{1,0:T(8,128)(2,1)S(1)}, bf16[256,1536]{1,0:T(8,128)(2,1)S(1)}, u32[]{:S(2)}, u32[]{:S(2)}) collective-permute-start(bf16[256,1536]{1,0:T(8,128)(2,1)S(1)} %slice.96), channel_id=1, source_target_pairs={{0,1},{1,0},{2,3},{3,2},{4,5},{5,4},{6,7},{7,6},{8,9},{9,8},{10,11... | collective-permute-start | bytes 2359304 | tf_op jit(solution)/shard_map/ppermute | solution.py:319
  291.5 189.7 %reduce-scatter.5.cloned.1.call-start = ((), (), s32[]{:S(2)}) async-start(), calls=%async_computation.9 | async-start | bytes 5750784 | tf_op jit(solution)/shard_map/reduce_scatter | solution.py:482
  291.5 58.9 %slice-start = ((s8[5505024]{0:T(1024)(128)(4,1)}), s8[4194304]{0:T(1024)(128)(4,1)S(1)}, s32[]{:S(2)}) async-start(s8[5505024]{0:T(1024)(128)(4,1)} %bitcast.79), calls=%async_computation.16 | async-start | bytes 8388608
  320.2 30.3 %slice-start.1 = ((s8[5505024]{0:T(1024)(128)(4,1)}), s8[1310720]{0:T(1024)(128)(4,1)S(1)}, s32[]{:S(2)}) async-start(s8[5505024]{0:T(1024)(128)(4,1)} %bitcast.79), calls=%async_computation.17 | async-start | bytes 2621440
  360.6 150.2 %reduce-scatter.9.cloned.1.call-start = ((), (), s32[]{:S(2)}) async-start(), calls=%async_computation.12 | async-start | bytes 14155776 | tf_op jit(solution)/shard_map/reduce_scatter | solution.py:474
  373.7 202.6 %reduce-scatter.11.cloned.1.call-start = ((), (), s32[]{:S(2)}) async-start(), calls=%async_computation.13 | async-start | bytes 7077888 | tf_op jit(solution)/shard_map/reduce_scatter | solution.py:475
  382.3 252.6 %all-reduce.2.cloned.1.call-start = ((), (), s32[]{:S(2)}) async-start(), calls=%async_computation.11 | async-start | bytes 1179648 | tf_op jit(solution)/shard_map/psum | solution.py:517
  394.9 18.4 %collective-permute-start.10 = (bf16[256,1536]{1,0:T(8,128)(2,1)S(1)}, bf16[256,1536]{1,0:T(8,128)(2,1)S(1)}, u32[]{:S(2)}, u32[]{:S(2)}) collective-permute-start(bf16[256,1536]{1,0:T(8,128)(2,1)S(1)} %get-tuple-element.30), channel_id=1, source_target_pairs={{0,1},{1,2},{2,3},{4,5},{5,6},{6,7},{8,9},{9,10},{10,11},{12,13},{... | collective-permute-start | bytes 2359304 | tf_op jit(solution)/shard_map/ppermute | solution.py:351
  397.9 21.6 %collective-permute-start.13 = (bf16[256,1536]{1,0:T(8,128)(2,1)S(1)}, bf16[256,1536]{1,0:T(8,128)(2,1)S(1)}, u32[]{:S(2)}, u32[]{:S(2)}) collective-permute-start(bf16[256,1536]{1,0:T(8,128)(2,1)S(1)} %get-tuple-element.31), channel_id=1, source_target_pairs={{1,0},{2,1},{3,2},{5,4},{6,5},{7,6},{9,8},{10,9},{11,10},{13,12},{... | collective-permute-start | bytes 2359304 | tf_op jit(solution)/shard_map/ppermute | solution.py:354
  415.0 19.1 %collective-permute-start.11 = (bf16[256,1536]{1,0:T(8,128)(2,1)S(1)}, bf16[256,1536]{1,0:T(8,128)(2,1)S(1)}, u32[]{:S(2)}, u32[]{:S(2)}) collective-permute-start(bf16[256,1536]{1,0:T(8,128)(2,1)S(1)} %add_convert_fusion.5), channel_id=1, source_target_pairs={{0,1},{1,2},{2,3},{4,5},{5,6},{6,7},{8,9},{9,10},{10,11},{12,13},{... | collective-permute-start | bytes 2359304 | tf_op jit(solution)/shard_map/ppermute | solution.py:351
  438.1 22.9 %copy-start.5 = (bf16[256,1536]{1,0:T(8,128)(2,1)S(1)}, bf16[256,1536]{1,0:T(8,128)(2,1)}, u32[]{:S(2)}) copy-start(bf16[256,1536]{1,0:T(8,128)(2,1)} %param.11) | copy-start | bytes 2359300
  438.1 19.0 %collective-permute-start.14 = (bf16[256,1536]{1,0:T(8,128)(2,1)S(1)}, bf16[256,1536]{1,0:T(8,128)(2,1)S(1)}, u32[]{:S(2)}, u32[]{:S(2)}) collective-permute-start(bf16[256,1536]{1,0:T(8,128)(2,1)S(1)} %get-tuple-element.29), channel_id=1, source_target_pairs={{1,0},{2,1},{3,2},{5,4},{6,5},{7,6},{9,8},{10,9},{11,10},{13,12},{... | collective-permute-start | bytes 2359304 | tf_op jit(solution)/shard_map/ppermute | solution.py:354
  439.8 1.2 collective-permute-start.16
  441.0 3.7 collective-permute-start.17
  444.7 3.6 collective-permute-start.18
  448.3 13.0 %collective-permute-start.19 = (f32[3,128]{1,0:T(4,128)S(1)}, f32[3,128]{1,0:T(4,128)S(1)}, u32[]{:S(2)}, u32[]{:S(2)}) collective-permute-start(f32[3,128]{1,0:T(4,128)S(1)} %add.201), channel_id=1, source_target_pairs={{0,1},{1,0},{2,3},{3,2},{4,5},{5,4},{6,7},{7,6},{8,9},{9,8},{10,11... | collective-permute-start | bytes 4616 | tf_op jit(solution)/shard_map/ppermute | solution.py:319
  451.3 61.9 %collective-permute-start.12 = (bf16[256,1536]{1,0:T(8,128)(2,1)}, bf16[256,1536]{1,0:T(8,128)(2,1)S(1)}, u32[]{:S(2)}, u32[]{:S(2)}) collective-permute-start(bf16[256,1536]{1,0:T(8,128)(2,1)} %get-tuple-element.28), channel_id=1, source_target_pairs={{0,1},{1,2},{2,3},{4,5},{5,6},{6,7},{8,9},{9,10},{10,11},{12,13},{... | collective-permute-start | bytes 2359304 | tf_op jit(solution)/shard_map/ppermute | solution.py:351
  453.3 273.8 %all-gather.16.cloned.1.call-start = ((), (), s32[]{:S(2)}) async-start(), calls=%async_computation.15 | async-start | bytes 3194880 | tf_op jit(solution)/shard_map/all_gather | solution.py:518
  459.6 119.2 %copy-start.7 = (f32[256,1536]{1,0:T(8,128)S(1)}, f32[256,1536]{1,0:T(8,128)}, u32[]{:S(2)}) copy-start(f32[256,1536]{1,0:T(8,128)} %copy-done.6) | copy-start | bytes 4718596
  459.6 53.7 %collective-permute-start.15 = (bf16[256,1536]{1,0:T(8,128)(2,1)}, bf16[256,1536]{1,0:T(8,128)(2,1)}, u32[]{:S(2)}, u32[]{:S(2)}) collective-permute-start(bf16[256,1536]{1,0:T(8,128)(2,1)} %add_convert_fusion.2), channel_id=1, source_target_pairs={{1,0},{2,1},{3,2},{5,4},{6,5},{7,6},{9,8},{10,9},{11,10},{13,12},{... | collective-permute-start | bytes 2359304 | tf_op jit(solution)/shard_map/ppermute | solution.py:354
  461.3 19.9 %collective-permute-start.20 = (f32[3,128]{1,0:T(4,128)S(1)}, f32[3,128]{1,0:T(4,128)S(1)}, u32[]{:S(2)}, u32[]{:S(2)}) collective-permute-start(f32[3,128]{1,0:T(4,128)S(1)} %add.202), channel_id=1, source_target_pairs={{0,2},{1,3},{2,0},{3,1},{4,6},{5,7},{6,4},{7,5},{8,10},{9,11},{10,... | collective-permute-start | bytes 4616 | tf_op jit(solution)/shard_map/ppermute | solution.py:319
  510.8 129.3 %collective-permute-start.21 = (bf16[192,4096]{1,0:T(8,128)(2,1)}, bf16[192,4096]{1,0:T(8,128)(2,1)}, u32[]{:S(2)}, u32[]{:S(2)}) collective-permute-start(bf16[192,4096]{1,0:T(8,128)(2,1)} %reduce-scatter.9.cloned.1.call-done), channel_id=1, source_target_pairs={{0,2},{1,3},{2,0},{3,1},{4,6},{5,7},{6,4},{7,5},{8,10},{9,11},{10,... | collective-permute-start | bytes 4718600 | tf_op jit(solution)/shard_map/ppermute | solution.py:319
  576.4 60.7 %collective-permute-start.23 = (bf16[256,1536]{1,0:T(8,128)(2,1)}, bf16[256,1536]{1,0:T(8,128)(2,1)}, u32[]{:S(2)}, u32[]{:S(2)}) collective-permute-start(bf16[256,1536]{1,0:T(8,128)(2,1)} %reduce-scatter.11.cloned.1.call-done), channel_id=1, source_target_pairs={{0,2},{1,3},{2,0},{3,1},{4,6},{5,7},{6,4},{7,5},{8,10},{9,11},{10,... | collective-permute-start | bytes 2359304 | tf_op jit(solution)/shard_map/ppermute | solution.py:319
  582.2 58.0 %copy-start.12 = (bf16[192,4096]{1,0:T(8,128)(2,1)S(1)}, bf16[192,4096]{1,0:T(8,128)(2,1)}, u32[]{:S(2)}) copy-start(bf16[192,4096]{1,0:T(8,128)(2,1)} %reduce-scatter.9.cloned.1.call-done) | copy-start | bytes 4718596
  638.6 46.2 %collective-permute-start.24 = (bf16[256,1536]{1,0:T(8,128)(2,1)S(1)}, bf16[256,1536]{1,0:T(8,128)(2,1)S(1)}, u32[]{:S(2)}, u32[]{:S(2)}) collective-permute-start(bf16[256,1536]{1,0:T(8,128)(2,1)S(1)} %add_convert_fusion.1), channel_id=1, source_target_pairs={{0,1},{1,0},{2,3},{3,2},{4,5},{5,4},{6,7},{7,6},{8,9},{9,8},{10,11... | collective-permute-start | bytes 2359304 | tf_op jit(solution)/shard_map/ppermute | solution.py:319
  643.3 113.2 %collective-permute-start.22 = (bf16[192,4096]{1,0:T(8,128)(2,1)}, bf16[192,4096]{1,0:T(8,128)(2,1)}, u32[]{:S(2)}, u32[]{:S(2)}) collective-permute-start(bf16[192,4096]{1,0:T(8,128)(2,1)} %add_convert_fusion), channel_id=1, source_target_pairs={{0,1},{1,0},{2,3},{3,2},{4,5},{5,4},{6,7},{7,6},{8,9},{9,8},{10,11... | collective-permute-start | bytes 4718600 | tf_op jit(solution)/shard_map/ppermute | solution.py:319
  768.7 14.1 %copy-start.1 = (bf16[512,1536]{1,0:T(8,128)(2,1)S(1)}, bf16[512,1536]{1,0:T(8,128)(2,1)}, u32[]{:S(2)}) copy-start(bf16[512,1536]{1,0:T(8,128)(2,1)} %param.20) | copy-start | bytes 4718596
  (18 other events, 101.5 us)
Sparse Core Ops, SparseCore 0:
  19.1 43.2 all-gather.7
  64.3 38.9 all-gather.9
  105.7 72.1 all-gather.11
  180.2 45.5 all-gather.13
  291.6 53.8 reduce-scatter.6
  360.7 53.7 reduce-scatter.4
  418.4 92.3 reduce-scatter.8
  514.6 61.7 reduce-scatter.10
  578.7 56.1 all-reduce.1
  636.3 90.7 all-gather.15

commit v2 on v1

--- a/solution.py
+++ b/solution.py
@@ -304,6 +304,106 @@
     )(projected, projected, projected, projected, projected, bias, gains, attended, shift, grad)
 
 
+def pack_kernel(at_ref, proj_ref, tail_ref, in_ref, packed_ref, own_ref, send_ref, sems,
+                seq_parts, wide, blocks):
+    seq_at, own, send = at_ref[0], at_ref[1], at_ref[2]
+    copies = []
+
+    def copy(source, target):
+        copies.append(pltpu.make_async_copy(source, target, sems.at[len(copies)]))
+
+    for kind in range(4):
+        at = pl.multiple_of(kind * seq_parts * wide + seq_at * wide, LANES)
+        copy(proj_ref.at[:, pl.ds(at, wide)], packed_ref.at[:, pl.ds(kind * wide, wide)])
+    copy(tail_ref, packed_ref.at[:, pl.ds(4 * wide, LANES)])
+    for block in range(blocks):
+        for target, quarter in ((own_ref, own), (send_ref, send)):
+            at = pl.multiple_of((block * 4 + quarter) * LANES, LANES)
+            copy(in_ref.at[:, pl.ds(at, LANES)], target.at[:, pl.ds(block * LANES, LANES)])
+    for item in copies:
+        item.start()
+    for item in copies:
+        item.wait()
+
+
+def pack(w_proj, tail, w_in, seq_at, own, send, seq_parts, quarter_rows):
+    rows, hidden = w_in.shape[0], w_in.shape[1]
+    wide = w_proj.shape[1] // 4 // seq_parts
+    if quarter_rows % LANES:
+        local = lax.dynamic_index_in_dim(
+            w_proj.reshape(rows, 4, seq_parts, wide), seq_at, 2, False
+        ).reshape(rows, 4 * wide)
+        folded = w_in.reshape(rows, -1, 4, quarter_rows)
+        return (
+            jnp.concatenate([local, tail], axis=1),
+            lax.dynamic_index_in_dim(folded, own, 2, False).reshape(rows, hidden // 4),
+            lax.dynamic_index_in_dim(folded, send, 2, False).reshape(rows, hidden // 4),
+        )
+    blocks = hidden // 4 // LANES
+    anywhere = pl.BlockSpec(memory_space=pl.ANY)
+    return pl.pallas_call(
+        partial(pack_kernel, seq_parts=seq_parts, wide=wide, blocks=blocks),
+        grid_spec=pltpu.PrefetchScalarGridSpec(
+            num_scalar_prefetch=1,
+            grid=(1,),
+            in_specs=[anywhere] * 3,
+            out_specs=[anywhere] * 3,
+            scratch_shapes=[pltpu.SemaphoreType.DMA((5 + 2 * blocks,))],
+        ),
+        out_shape=[
+            jax.ShapeDtypeStruct((rows, 4 * wide + LANES), jnp.bfloat16),
+            jax.ShapeDtypeStruct((rows, hidden // 4), jnp.bfloat16),
+            jax.ShapeDtypeStruct((rows, hidden // 4), jnp.bfloat16),
+        ],
+        compiler_params=pltpu.CompilerParams(vmem_limit_bytes=4 * 2**20),
+        cost_estimate=pl.CostEstimate(flops=0, transcendentals=0, bytes_accessed=rows * hidden * 2),
+        name="pack",
+    )(jnp.stack([seq_at, own, send]), w_proj, tail, w_in)
+
+
+def spread_kernel(piece_ref, weight_ref, out_ref, sum_ref):
+    @pl.when((pl.program_id(0) == 0) & (pl.program_id(1) == 0))
+    def _():
+        sum_ref[...] = jnp.zeros_like(sum_ref)
+
+    total = sum_ref[...]
+    wide = piece_ref.shape[2]
+    for quarter in range(4):
+        columns = slice(quarter * wide, (quarter + 1) * wide)
+        piece = piece_ref[quarter].astype(jnp.float32)
+        out_ref[:, columns] = piece
+        product = piece * weight_ref[:, columns].astype(jnp.float32)
+        for lane in range(0, wide, LANES):
+            total = total + product[:, lane : lane + LANES]
+    sum_ref[...] = total
+
+
+def spread(pieces, weight, groups, wide):
+    rows = weight.shape[0]
+    per_group = weight.shape[1] // groups // (4 * wide)
+    return pl.pallas_call(
+        spread_kernel,
+        grid=(groups, per_group),
+        in_specs=[
+            pl.BlockSpec((4, rows, wide), lambda g, f: (g, 0, f)),
+            pl.BlockSpec((rows, 4 * wide), lambda g, f: (0, g * per_group + f)),
+        ],
+        out_specs=[
+            pl.BlockSpec((rows, 4 * wide), lambda g, f: (0, g * per_group + f)),
+            pl.BlockSpec((rows, LANES), lambda g, f: (0, 0)),
+        ],
+        out_shape=[
+            jax.ShapeDtypeStruct(weight.shape, jnp.float32),
+            jax.ShapeDtypeStruct((rows, LANES), jnp.float32),
+        ],
+        compiler_params=pltpu.CompilerParams(vmem_limit_bytes=32 * 2**20),
+        cost_estimate=pl.CostEstimate(
+            flops=weight.size * 2, transcendentals=0, bytes_accessed=weight.size * 8
+        ),
+        name="spread",
+    )(pieces, weight)
+
+
 def inverse_norm(values):
     return lax.rsqrt(jnp.mean(values * values, axis=-1, keepdims=True) + epsilon)
 
@@ -317,6 +417,10 @@
 def swap_with(values, axis, bit):
     size = lax.axis_size(axis)
     return lax.ppermute(values, axis, [(i, i ^ bit) for i in range(size)])
+
+
+def swapped(flag, first, second):
+    return jnp.where(flag, second, first), jnp.where(flag, first, second)
 
 
 def line_gather(block, axis):
@@ -340,7 +444,9 @@
     rows = partial_rows.shape[0] // size
 
     def part(at):
-        return lax.dynamic_slice_in_dim(partial_rows, jnp.clip(at, 0, size - 1) * rows, rows, 0)
+        return lax.dynamic_slice_in_dim(
+            partial_rows, jnp.clip(at, 0, size - 1) * rows, rows, 0
+        ).astype(jnp.float32)
 
     up = down = None
     for step in range(1, size):
@@ -364,6 +470,69 @@
             values = values + swap_with(values, axis, bit)
             bit *= 2
     return values
+
+
+def added(first, second):
+    return (first.astype(jnp.float32) + second.astype(jnp.float32)).astype(jnp.bfloat16)
+
+
+def plane_gather(block):
+    pairs = lax.axis_size("fsdp") // 2
+    if pairs == 4:
+        half = block.shape[0] // 2
+        beside = swap_with(block, "fsdp", 2)
+        across = swap_with(block, "fsdp", 4)
+        corner = [swap_with(beside[:half], "fsdp", 4), swap_with(across[half:], "fsdp", 2)]
+        return [block, beside, across, jnp.concatenate(corner, axis=0)]
+    parts = [block]
+    bit = 2
+    while bit < 2 * pairs:
+        moved = swap_with(jnp.stack(parts), "fsdp", bit)
+        parts = parts + [moved[i] for i in range(len(parts))]
+        bit *= 2
+    return parts
+
+
+def plane_scatter(parts):
+    if len(parts) == 4:
+        own, beside, across, corner = parts
+        half = own.shape[0] // 2
+        from_beside = swap_with(corner[:half], "fsdp", 2)
+        from_across = swap_with(corner[half:], "fsdp", 4)
+        across = jnp.concatenate([added(across[:half], from_beside), across[half:]], axis=0)
+        beside = jnp.concatenate([beside[:half], added(beside[half:], from_across)], axis=0)
+        beside = swap_with(beside, "fsdp", 2)
+        across = swap_with(across, "fsdp", 4)
+        total = own.astype(jnp.float32) + beside.astype(jnp.float32) + across.astype(jnp.float32)
+        return total.astype(jnp.bfloat16)
+    while len(parts) > 1:
+        half = len(parts) // 2
+        moved = swap_with(jnp.stack(parts[half:]), "fsdp", 2 * half)
+        parts = [added(parts[i], moved[i]) for i in range(half)]
+    return parts[0]
+
+
+def in_order(parts, place):
+    count = len(parts)
+    bit = 1
+    while bit < count:
+        flag = (place // bit) % 2 == 1
+        parts = [jnp.where(flag, parts[k ^ bit], parts[k]) for k in range(count)]
+        bit *= 2
+    return parts
+
+
+def group_gather(block):
+    along = swap_with(block, "seq", 1)
+    return [block, swap_with(block, "fsdp", 1), along, swap_with(along, "fsdp", 1)]
+
+
+def group_scatter(parts):
+    sent = swap_with(jnp.concatenate([parts[1], parts[3]], axis=0), "fsdp", 1)
+    rows = parts[0].shape[0]
+    own = parts[0].astype(jnp.float32) + sent[:rows].astype(jnp.float32)
+    along = added(parts[2], sent[rows:])
+    return own + swap_with(along, "seq", 1).astype(jnp.float32)
 
 
 def body(
@@ -384,26 +553,26 @@
     seq_parts = lax.axis_size("seq")
     fsdp_parts = lax.axis_size("fsdp")
     seq_at = lax.axis_index("seq")
-    side = seq_at % 2
+    fsdp_at = lax.axis_index("fsdp")
+    core = fsdp_at % 2
+    place = fsdp_at // 2
+    places = fsdp_parts // 2
+    chip_rows = 2 * weight_rows
+    quarter = 2 * (seq_at % 2) + core
     head_count = forget_bias.shape[0]
     head_width = qk_gain.shape[1]
     heads = head_count // seq_parts
     wide = heads * head_width
     small_wide = 3 * heads
-    length = row_count * seq_parts
-    hidden_rows = w_down.shape[0]
-    hidden_half = fsdp_parts * hidden_rows // 2
+    quarter_rows = w_down.shape[0] // 4
+    hidden = fsdp_parts * quarter_rows
 
     every_input = line_gather(inputs, "seq")
-    local_proj = lax.dynamic_index_in_dim(
-        w_proj.reshape(weight_rows, 4, seq_parts, wide), seq_at, 2, False
-    ).reshape(weight_rows, 4 * wide)
     local_small = lax.dynamic_index_in_dim(
         w_small.reshape(weight_rows, 3, seq_parts, heads), seq_at, 2, False
     ).reshape(weight_rows, small_wide)
-    packed = jnp.concatenate(
+    tail = jnp.concatenate(
         [
-            local_proj,
             local_small,
             norm_attn[:, None],
             norm_ffn[:, None],
@@ -411,19 +580,26 @@
         ],
         axis=1,
     )
+    packed, own_in, send_in = pack(
+        w_proj, tail, w_in, seq_at, quarter, quarter ^ 1, seq_parts, quarter_rows
+    )
     packed_full = lax.all_gather(packed, "fsdp", axis=0, tiled=True)
     gain_attention = packed_full[:, 4 * wide + small_wide].astype(jnp.float32)
     gain_ffn = packed_full[:, 4 * wide + small_wide + 1].astype(jnp.float32)
     out_full = lax.all_gather(w_out, "fsdp", axis=0, tiled=True)
-    in_half = lax.dynamic_index_in_dim(
-        w_in.reshape(weight_rows, 2, fsdp_parts, 2, hidden_rows // 2), side, 3, False
-    ).reshape(weight_rows, 2 * hidden_half)
-    in_half = lax.all_gather(in_half, "fsdp", axis=0, tiled=True)
-    down_half = lax.dynamic_index_in_dim(
-        w_down.reshape(2, hidden_rows // 2, model_width), side, 0, False
-    )
-    down_half = lax.all_gather(down_half, "fsdp", axis=0, tiled=True)
-    cotangent_pair = jnp.concatenate([cotangent, swap_with(cotangent, "seq", 1)], axis=0)
+
+    def chip_block(own, send):
+        return jnp.concatenate(swapped(core == 1, own, swap_with(send, "fsdp", 1)), axis=0)
+
+    in_parts = plane_gather(chip_block(own_in, send_in))
+    in_full = jnp.concatenate(in_parts, axis=0)
+    own_down = lax.dynamic_slice_in_dim(w_down, quarter * quarter_rows, quarter_rows, 0)
+    send_down = lax.dynamic_slice_in_dim(w_down, (quarter ^ 1) * quarter_rows, quarter_rows, 0)
+    down_parts = plane_gather(chip_block(own_down, send_down))
+    down_full = jnp.concatenate(in_order(down_parts, place), axis=0)
+
+    late_cotangent, every_input = lax.optimization_barrier((cotangent, every_input))
+    cotangent_group = jnp.concatenate(group_gather(late_cotangent), axis=0)
 
     wide_input = every_input.astype(jnp.float32)
     normed = (wide_input * inverse_norm(wide_input) * gain_attention).astype(jnp.bfloat16)
@@ -435,52 +611,90 @@
     gated, attended, shift = attend(projected, bias_lanes, gain_lanes, heads)
     mixed_rows = lax.all_to_all(gated, "seq", split_axis=0, concat_axis=1, tiled=True)
 
+    def features_by_place(values):
+        blocks = [values[:, k * chip_rows : (k + 1) * chip_rows] for k in range(places)]
+        return jnp.concatenate(in_order(blocks, place), axis=1)
+
     source = inputs.astype(jnp.float32)
     residual = source + dot_ab(mixed_rows, out_full)
     factor_ffn = inverse_norm(residual)
-    unit_ffn = residual * factor_ffn
-    normed_ffn = (unit_ffn * gain_ffn).astype(jnp.bfloat16)
-    normed_pair = jnp.concatenate([normed_ffn, swap_with(normed_ffn, "seq", 1)], axis=0)
-    gate_up = dot_ab(normed_pair, in_half)
-    gate_part = gate_up[:, :hidden_half]
-    up_part = gate_up[:, hidden_half:]
+    normed_ffn = (residual * factor_ffn * gain_ffn).astype(jnp.bfloat16)
+    normed_group = jnp.concatenate(group_gather(features_by_place(normed_ffn)), axis=0)
+    gate_up = dot_ab(normed_group, in_full)
+    gate_part = gate_up[:, :hidden]
+    up_part = gate_up[:, hidden:]
     inner_sigmoid = jax.nn.sigmoid(gate_part)
     silu_gate = gate_part * inner_sigmoid
     activated = (silu_gate * up_part).astype(jnp.bfloat16)
-    down_part = dot_ab(activated, down_half)
-    output = (
-        residual
-        + down_part[:row_count]
-        + swap_with(down_part[row_count:].astype(jnp.bfloat16), "seq", 1).astype(jnp.float32)
-    ).astype(jnp.bfloat16)
-
-    grad_act = dot_abt(cotangent_pair, down_half)
+
+    def by_rows(values):
+        values = values.astype(jnp.bfloat16)
+        return [values[k * row_count : (k + 1) * row_count] for k in range(4)]
+
+    output = (residual + group_scatter(by_rows(dot_ab(activated, down_full)))).astype(jnp.bfloat16)
+
+    grad_act = dot_abt(cotangent_group, down_full)
     grad_gate = grad_act * up_part * inner_sigmoid * (1.0 + gate_part * (1.0 - inner_sigmoid))
     grad_up = grad_act * silu_gate
     grad_gate_up = jnp.concatenate([grad_gate, grad_up], axis=1).astype(jnp.bfloat16)
-    back_part = dot_abt(grad_gate_up, in_half)
-    grad_normed_ffn = back_part[:row_count] + swap_with(
-        back_part[row_count:].astype(jnp.bfloat16), "seq", 1
-    ).astype(jnp.float32)
+    grad_normed_ffn = features_by_place(group_scatter(by_rows(dot_abt(grad_gate_up, in_full))))
     grad_residual = cotangent.astype(jnp.float32) + norm_back(
         residual, factor_ffn, grad_normed_ffn * gain_ffn
     )
     grad_branch = grad_residual.astype(jnp.bfloat16)
     grad_mixed = dot_abt(grad_branch, out_full).astype(jnp.bfloat16)
     grad_heads = lax.all_to_all(grad_mixed, "seq", split_axis=1, concat_axis=0, tiled=True)
-    grad_down = dot_atb(activated, cotangent_pair).astype(jnp.bfloat16)
-    grad_in = dot_atb(normed_pair, grad_gate_up).astype(jnp.bfloat16)
+
+    grad_in = dot_atb(normed_group, grad_gate_up).astype(jnp.bfloat16)
+    grad_down = dot_atb(activated, cotangent_group).astype(jnp.bfloat16)
     grad_out = dot_atb(mixed_rows, grad_branch).astype(jnp.bfloat16)
-    grad_in = lax.psum_scatter(grad_in, "fsdp", scatter_dimension=0, tiled=True)
-    grad_down = lax.psum_scatter(grad_down, "fsdp", scatter_dimension=0, tiled=True)
+    grad_in = plane_scatter([grad_in[k * chip_rows : (k + 1) * chip_rows] for k in range(places)])
+    grad_down = grad_down.reshape(places, 2 * quarter_rows, model_width)
+    grad_down = plane_scatter(
+        [lax.dynamic_index_in_dim(grad_down, place ^ k, 0, False) for k in range(places)]
+    )
+
+    def both_quarters(block):
+        rows = block.shape[0] // 2
+        own = lax.dynamic_slice_in_dim(block, core * rows, rows, 0)
+        sent = lax.dynamic_slice_in_dim(block, (1 - core) * rows, rows, 0)
+        return jnp.stack(swapped(core == 1, own, swap_with(sent, "fsdp", 1)))
+
+    far = seq_at >= 2
+
+    def all_pieces(first, second):
+        keep, send = swapped(far, first, second)
+        return line_gather(added(keep, swap_with(send, "seq", 2))[None], "seq")
+
+    grad_in = both_quarters(grad_in)
+    grad_in = all_pieces(grad_in[:, :, :hidden], grad_in[:, :, hidden:])
+    grad_down = both_quarters(grad_down)
+    grad_down = all_pieces(
+        grad_down[:, : quarter_rows // 2], grad_down[:, quarter_rows // 2 :]
+    )
+    grad_down = (
+        grad_down.reshape(2, 2, 2, quarter_rows // 2, model_width)
+        .transpose(1, 2, 0, 3, 4)
+        .reshape(4 * quarter_rows, model_width)
+        .astype(jnp.float32)
+    )
     grad_out = lax.psum_scatter(grad_out, "fsdp", scatter_dimension=0, tiled=True)
+    grad_out = lax.psum(grad_out, "seq").astype(jnp.float32)
 
     grad_projected, gain_sums, forget_sums = attend_back(
         projected, bias_lanes, gain_lanes, attended, shift, grad_heads, heads
     )
     grad_packed = dot_atb(normed, grad_projected).astype(jnp.bfloat16)
-    grad_packed = lax.psum_scatter(grad_packed, "fsdp", scatter_dimension=0, tiled=True)
-    grad_normed = line_scatter(dot_abt(grad_projected, packed_full), "seq")
+    grad_packed = grad_packed.reshape(places, 2, weight_rows, 4 * wide + LANES)
+    grad_packed = added(
+        lax.dynamic_index_in_dim(grad_packed, core, 1, False),
+        swap_with(lax.dynamic_index_in_dim(grad_packed, 1 - core, 1, False), "fsdp", 1),
+    )
+    grad_packed = plane_scatter(
+        [lax.dynamic_index_in_dim(grad_packed, place ^ k, 0, False) for k in range(places)]
+    )
+    every_packed = line_gather(grad_packed[None], "seq")
+    grad_normed = line_scatter(dot_abt(grad_projected, packed_full).astype(jnp.bfloat16), "seq")
     grad_inputs = grad_residual + norm_back(
         source, inverse_norm(source), grad_normed * gain_attention
     )
@@ -495,44 +709,30 @@
     grad_qk_gain = sums[:2, :head_width] + sums[:2, head_width:]
     grad_forget_bias = sums[2, :head_count]
 
-    def whole_hidden(half):
-        total = half.astype(jnp.float32)
-        bit = 2
-        while bit < seq_parts:
-            moved = swap_with(total.astype(jnp.bfloat16), "seq", bit).astype(jnp.float32)
-            total = total + moved
-            bit *= 2
-        total = total.astype(jnp.bfloat16)
-        other = swap_with(total, "seq", 1)
-        first = jnp.where(side == 0, total, other)
-        second = jnp.where(side == 0, other, total)
-        return first.astype(jnp.float32), second.astype(jnp.float32)
-
-    first, second = whole_hidden(grad_in)
-    folded = (weight_rows, 2, fsdp_parts, 1, hidden_rows // 2)
-    grad_in = jnp.concatenate([first.reshape(folded), second.reshape(folded)], axis=3).reshape(
-        weight_rows, 4 * hidden_half
-    )
-    grad_down = jnp.concatenate(whole_hidden(grad_down), axis=0)
-    grad_out = lax.psum(grad_out, "seq").astype(jnp.float32)
-    every_packed = lax.all_gather(grad_packed, "seq", axis=0, tiled=False).astype(jnp.float32)
-    grad_proj = jnp.moveaxis(
-        every_packed[:, :, : 4 * wide].reshape(seq_parts, weight_rows, 4, wide), 0, 2
-    ).reshape(weight_rows, 4 * seq_parts * wide)
     grad_small = jnp.moveaxis(
-        every_packed[:, :, 4 * wide : 4 * wide + small_wide].reshape(
-            seq_parts, weight_rows, 3, heads
-        ),
+        every_packed[:, :, 4 * wide : 4 * wide + small_wide]
+        .astype(jnp.float32)
+        .reshape(seq_parts, weight_rows, 3, heads),
         0,
         2,
     ).reshape(weight_rows, 3 * head_count)
+    if quarter_rows % LANES or wide % LANES:
+        folded = grad_in.reshape(2, 4, weight_rows, fsdp_parts, quarter_rows)
+        grad_in = folded.transpose(2, 0, 3, 1, 4).reshape(w_in.shape).astype(jnp.float32)
+        folded = every_packed[:, :, : 4 * wide].reshape(seq_parts, weight_rows, 4, wide)
+        grad_proj = folded.transpose(1, 2, 0, 3).reshape(w_proj.shape).astype(jnp.float32)
+        in_sums = grad_in * w_in.astype(jnp.float32)
+        proj_sums = grad_proj * w_proj.astype(jnp.float32)
+    else:
+        grad_in, in_sums = spread(
+            grad_in.reshape(8, weight_rows, hidden), w_in, 2, quarter_rows
+        )
+        grad_proj, proj_sums = spread(every_packed, w_proj, 1, wide)
     grad_gain_attention = (
-        jnp.sum(grad_proj * w_proj.astype(jnp.float32), axis=1)
+        jnp.sum(proj_sums, axis=1)
         + jnp.sum(grad_small * w_small.astype(jnp.float32), axis=1)
     ) / norm_attn.astype(jnp.float32)
-    grad_gain_ffn = jnp.sum(grad_in * w_in.astype(jnp.float32), axis=1) / norm_ffn.astype(
-        jnp.float32
-    )
+    grad_gain_ffn = jnp.sum(in_sums, axis=1) / norm_ffn.astype(jnp.float32)
     return (
         output,
         grad_inputs,

time: 797 us -> 684 us (0.86)
  waiting for transfers between devices: 404 us -> 239 us
  starting transfers between devices: 61.5 us -> 163 us
  local copies, waits for them, and re-layouts: 96.8 us -> 62.9 us
  blocking collectives: 24.2 us -> 0 us
  Pallas kernels: 45.9 us -> 58.2 us
  matrix products: 103 us -> 90.7 us
  other arithmetic: 39.4 us -> 48.8 us
    reduce_scatter x3 -> x0, waiting for transfers between devices: 89.4 us -> none  [the longest x1 60.9 us: body(): lax.psum_scatter(grad_down, 'fsdp', scatter_dimension=0, tiled=True)]
    all_gather x3 -> x0, waiting for transfers between devices: 60.8 us -> none  [the longest x1 40 us: body(): lax.all_gather(grad_packed, 'seq', axis=0, tiled=False).astype(jnp.float32)]
    reshape x7 -> x0, local copies, waits for them, and re-layouts: 48.9 us -> none  [the longest x2 18 us: body(): jnp.concatenate([first.reshape(folded), second.reshape(folded)], axis=3)]
    ppermute x3 -> x12, starting transfers between devices: 15.8 us -> 61.8 us  [line_gather(): up = lax.ppermute(up, axis, [(i, i + 1) for i in range(size - 1)])]
    ppermute x3 -> x12, waiting for transfers between devices: 41.6 us -> 80.7 us  [line_gather(): up = lax.ppermute(up, axis, [(i, i + 1) for i in range(size - 1)])]
    ppermute x13 -> x42, starting transfers between devices: 23.3 us -> 60.7 us  [swap_with(): return lax.ppermute(values, axis, [(i, i ^ bit) for i in range(size)])]
    all_to_all x1 -> x0, blocking collectives: 24.2 us -> none  [body(): lax.all_to_all(grad_mixed, 'seq', split_axis=1, concat_axis=0, tiled=True)]
    psum x1, waiting for transfers between devices: 52.7 us -> 31 us  [body(): grad_out = lax.psum(grad_out, 'seq').astype(jnp.float32)]
  transfers between devices with their start and end apart: 36 -> 78, of which waited for: 22 -> 25; matrix products, arithmetic and copies ran while one was open for 21% -> 22% of each run, Pallas kernels for 6% -> 8%
where the time goes in v2:
time: 684 us; the launch traced here: 677 us
  waiting for transfers between devices  239 us (35%)
  starting transfers between devices  163 us (24%)
  matrix products  90.7 us (13%)
  local copies, waits for them, and re-layouts  62.9 us (9%)
  Pallas kernels  58.2 us (9%)
  other arithmetic  48.8 us (7%)
  between operations  15.7 us (2%)
    ppermute x42, waiting for transfers between devices, swap_with(): return lax.ppermute(values, axis, [(i, i ^ bit) for i in range(size)])  95.3 us
    ppermute x12, waiting for transfers between devices, line_gather(): up = lax.ppermute(up, axis, [(i, i + 1) for i in range(size - 1)])  80.7 us
    ppermute x12, starting transfers between devices, line_gather(): up = lax.ppermute(up, axis, [(i, i + 1) for i in range(size - 1)])  61.8 us
    ppermute x42, starting transfers between devices, swap_with(): return lax.ppermute(values, axis, [(i, i ^ bit) for i in range(size)])  60.7 us
    unnamed x140, local copies, waits for them, and re-layouts  36.6 us
    dot_general x4, matrix products, dot_ab(): lax.dot_general(a, b, (((1,), (0,)), ((), ())), preferred_element_type=jn...  33 us
    dot_general x4, matrix products, dot_atb(): lax.dot_general(a, b, (((0,), (0,)), ((), ())), preferred_element_type=jn...  32.2 us
    psum x1, waiting for transfers between devices, body(): grad_out = lax.psum(grad_out, 'seq').astype(jnp.float32)  31 us
  transfers between devices with their start and end apart: 78, of which 25 were waited for; matrix products, arithmetic and copies ran while one was open for 22% of the time, Pallas kernels for 8%

profile of v2, /device:TPU:0, one launch (start us, length us, event | category | flops | bytes accessed | tf_op | source)
XLA Modules:
  0.0 677.5 jit_solution(13516421615084869318)
XLA Ops:
  15.4 5.8 collective-permute-start
  25.4 11.7 %collective-permute-done = bf16[256,1536]{1,0:T(8,128)(2,1)} collective-permute-done((bf16[256,1536]{1,0:T(8,128)(2,1)S(1)}, bf16[256,1536]{1,0:T(8,128)(2,1)}, u32[]{:S(2)}, u32[]{:S(2)}) %collective-permute-start) | collective-permute-done | bytes 786464 | tf_op jit(solution)/shard_map/ppermute | solution.py:433
  37.1 4.5 collective-permute-start.1
  48.6 9.2 %collective-permute-done.1 = bf16[256,1536]{1,0:T(8,128)(2,1)S(1)} collective-permute-done((bf16[256,1536]{1,0:T(8,128)(2,1)}, bf16[256,1536]{1,0:T(8,128)(2,1)S(1)}, u32[]{:S(2)}, u32[]{:S(2)}) %collective-permute-start.1) | collective-permute-done | bytes 786464 | tf_op jit(solution)/shard_map/ppermute | solution.py:433
  57.8 4.3 collective-permute-start.2
  66.0 8.7 %collective-permute-done.15 = bf16[256,1536]{1,0:T(8,128)(2,1)S(1)} collective-permute-done((bf16[256,1536]{1,0:T(8,128)(2,1)S(1)}, bf16[256,1536]{1,0:T(8,128)(2,1)S(1)}, u32[]{:S(2)}, u32[]{:S(2)}) %collective-permute-start.15) | collective-permute-done | bytes 786464 | tf_op jit(solution)/shard_map/ppermute | solution.py:419
  82.7 15.1 %collective-permute-done.5 = bf16[256,1536]{1,0:T(8,128)(2,1)S(1)} collective-permute-done((bf16[256,1536]{1,0:T(8,128)(2,1)S(1)}, bf16[256,1536]{1,0:T(8,128)(2,1)S(1)}, u32[]{:S(2)}, u32[]{:S(2)}) %collective-permute-start.5) | collective-permute-done | bytes 786464 | tf_op jit(solution)/shard_map/ppermute | solution.py:434
  102.8 10.5 %convolution_convert_fusion.5.q_ref.k_ref.v_ref.g_ref.small_ref = bf16[1024,1664]{1,0:T(8,128)(2,1)} fusion(bf16[1536,1664]{1,0:T(8,128)(2,1)} %all-gather.3.cloned.1.call-done, bf16[1024,1536]{1,0:T(8,128)(2,1)} %copy-done.9, f32[1536]{0:T(1024)S(1)} %get-tuple-element.42, f32[1024]{0:T(1024)S(1)} %add_rsqrt_fusion), kind=kOutput, calls=%fused_computation.18 | convolution fusion | flops 5242486784 | bytes 11675648 | tf_op jit(solution)/shard_map/dot_general | solution.py:16
  113.3 15.6 %attend.1 = (bf16[1024,384]{1,0:T(8,128)(2,1)S(1)}, bf16[1024,384]{1,0:T(8,128)(2,1)S(1)}, f32[1024,384]{1,0:T(8,128)S(1)}) custom-call(bf16[1024,1664]{1,0:T(8,128)(2,1)} %convolution_convert_fusion.5.q_ref.k_ref.v_ref.g_ref.small_ref, bf16[1024,1664]{1,0:T(8,128)(2,1)} %convolution_convert_fusion.5.q_ref.k_ref.v_ref.g_ref.small_ref, ...), custom_call_target="tpu_custom_call" | custom-call | flops 1610612736 | bytes 7864320 | tf_op jit(solution)/shard_map/attend/pallas_call | solution.py:254
  130.1 4.5 all-to-all-start
  139.2 4.3 broadcast_select_fusion.8
  161.9 5.1 collective-permute-done.22
  168.8 14.6 %collective-permute-done.7 = bf16[256,1536]{1,0:T(8,128)(2,1)S(1)} collective-permute-done((bf16[256,1536]{1,0:T(8,128)(2,1)S(1)}, bf16[256,1536]{1,0:T(8,128)(2,1)S(1)}, u32[]{:S(2)}, u32[]{:S(2)}) %collective-permute-start.7) | collective-permute-done | bytes 786464 | tf_op jit(solution)/shard_map/ppermute | solution.py:419
  188.6 14.7 %fusion.35 = f32[1024,2048]{1,0:T(8,128)} fusion(bf16[1536,2048]{1,0:T(8,128)(2,1)S(1)} %constant_dynamic-update-slice_fusion.7, bf16[256,1536]{1,0:T(8,128)(2,1)S(1)} %collective-permute-done.8, bf16[256,1536]{1,0:T(8,128)(2,1)S(1)} %collective-permute-done.7, bf16[256,1536]{1,0:T(8,128)(2,1)S(1)} %collective-permute-done.6, ...), kind=kOutput, calls=%fused_computation.211 | convolution fusion | flops 6464471040 | bytes 17825792 | tf_op jit(solution)/shard_map/dot_general | solution.py:16
  203.3 10.9 %multiply_convert_fusion.1 = (bf16[1024,1024]{1,0:T(8,128)(2,1)}, bf16[1024,1024]{1,0:T(8,128)(2,1)}, bf16[1024,1024]{1,0:T(8,128)(2,1)S(1)}) fusion(f32[1024,2048]{1,0:T(8,128)} %fusion.35, bf16[1024,1536]{1,0:T(8,128)(2,1)S(1)} %constant_dynamic-update-slice_fusion.15, bf16[256,1536]{1,0:T(8,128)(2,1)S(1)} %copy-done.27, ...), kind=kOutput, calls=%fused_computation.12 | convolution fusion | flops 3249537024 | bytes 20971520 | tf_op jit(solution)/shard_map/dot_general | solution.py:20
  221.8 7.1 %convolution_convert_fusion.3 = bf16[1024,1536]{1,0:T(8,128)(2,1)S(1)} fusion(bf16[1536,2048]{1,0:T(8,128)(2,1)S(1)} %copy-done.31, bf16[1024,1024]{1,0:T(8,128)(2,1)S(1)} %copy-done.48, bf16[1024,1024]{1,0:T(8,128)(2,1)S(1)} %copy-done.47), kind=kOutput, calls=%fused_computation.16 | convolution fusion | flops 6452412416 | bytes 13631488 | tf_op jit(solution)/shard_map/dot_general | solution.py:20
  234.2 13.9 %convolution_convert_fusion.1 = bf16[1536,2048]{1,0:T(8,128)(2,1)S(1)} fusion(bf16[1024,1024]{1,0:T(8,128)(2,1)} %get-tuple-element.48, bf16[1024,1024]{1,0:T(8,128)(2,1)} %get-tuple-element.47, bf16[256,1536]{1,0:T(8,128)(2,1)} %copy-done.45, bf16[256,1536]{1,0:T(8,128)(2,1)} %copy-done.43, bf16[256,1536]{1,0:T(8,128)(2,1)} %copy-done.44, ...), kind=kOutput, calls=%fused_computation.3 | convolution fusion | flops 6476005376 | bytes 13631488 | tf_op jit(solution)/shard_map/dot_general | solution.py:24
  253.2 15.7 %collective-permute-done.48 = bf16[192,2048]{1,0:T(8,128)(2,1)S(1)} collective-permute-done((bf16[192,2048]{1,0:T(8,128)(2,1)S(1)}, bf16[192,2048]{1,0:T(8,128)(2,1)S(1)}, u32[]{:S(2)}, u32[]{:S(2)}) %collective-permute-start.48) | collective-permute-done | bytes 786464 | tf_op jit(solution)/shard_map/ppermute | solution.py:419
  271.9 13.8 %collective-permute-done.63 = bf16[256,1536]{1,0:T(8,128)(2,1)S(1)} collective-permute-done((bf16[256,1536]{1,0:T(8,128)(2,1)S(1)}, bf16[256,1536]{1,0:T(8,128)(2,1)S(1)}, u32[]{:S(2)}, u32[]{:S(2)}) %collective-permute-start.63) | collective-permute-done | bytes 786464 | tf_op jit(solution)/shard_map/ppermute | solution.py:419
  294.6 20.6 %collective-permute-done.65 = bf16[2,64,1536]{2,1,0:T(8,128)(2,1)S(1)} collective-permute-done((bf16[2,64,1536]{2,1,0:T(8,128)(2,1)S(1)}, bf16[2,64,1536]{2,1,0:T(8,128)(2,1)S(1)}, u32[]{:S(2)}, u32[]{:S(2)}) %collective-permute-start.65) | collective-permute-done | bytes 393248 | tf_op jit(solution)/shard_map/ppermute | solution.py:419
  316.0 6.9 %collective-permute-start.66 = (bf16[1,2,64,1536]{3,2,1,0:T(8,128)(2,1)}, bf16[1,2,64,1536]{3,2,1,0:T(8,128)(2,1)}, u32[]{:S(2)}, u32[]{:S(2)}) collective-permute-start(bf16[1,2,64,1536]{3,2,1,0:T(8,128)(2,1)} %fusion.26), channel_id=1, source_target_pairs={{0,1},{1,2},{2,3},{4,5},{5,6},{6,7},{8,9},{9,10},{10,11},{12,13},{... | collective-permute-start | bytes 1179656 | tf_op jit(solution)/shard_map/ppermute | solution.py:433
  328.1 6.3 collective-permute-done.20
  339.8 4.5 all-to-all-start.1
  344.3 4.7 collective-permute-start.67
  350.3 5.2 convolution_convert_fusion.2
  355.6 9.5 %collective-permute-done.67 = bf16[1,2,64,1536]{3,2,1,0:T(8,128)(2,1)} collective-permute-done((bf16[1,2,64,1536]{3,2,1,0:T(8,128)(2,1)}, bf16[1,2,64,1536]{3,2,1,0:T(8,128)(2,1)}, u32[]{:S(2)}, u32[]{:S(2)}) %collective-permute-start.67) | collective-permute-done | bytes 393248 | tf_op jit(solution)/shard_map/ppermute | solution.py:433
  365.1 7.8 %collective-permute-start.68 = (bf16[1,2,64,1536]{3,2,1,0:T(8,128)(2,1)}, bf16[1,2,64,1536]{3,2,1,0:T(8,128)(2,1)S(1)}, u32[]{:S(2)}, u32[]{:S(2)}) collective-permute-start(bf16[1,2,64,1536]{3,2,1,0:T(8,128)(2,1)} %collective-permute-done.67), channel_id=1, source_target_pairs={{0,1},{1,2},{2,3},{4,5},{5,6},{6,7},{8,9},{9,10},{10,11},{12,13},{... | collective-permute-start | bytes 1179656 | tf_op jit(solution)/shard_map/ppermute | solution.py:433
  377.7 4.5 collective-permute-start.53
  391.9 30.2 %attend_back.1 = (bf16[1024,1664]{1,0:T(8,128)(2,1)}, f32[2,128]{1,0:T(2,128)S(1)}, f32[3,1,128]{2,1,0:T(1,128)S(1)}) custom-call(bf16[1024,1664]{1,0:T(8,128)(2,1)} %convolution_convert_fusion.5.q_ref.k_ref.v_ref.g_ref.small_ref, bf16[1024,1664]{1,0:T(8,128)(2,1)} %convolution_convert_fusion.5.q_ref.k_ref.v_ref.g_ref.small_ref, ...), custom_call_target="tpu_custom_call" | custom-call | flops 4026531840 | bytes 12582912 | tf_op jit(solution)/shard_map/attend_back/pallas_call | solution.py:278
  422.5 9.2 %convolution_convert_fusion = bf16[1536,1664]{1,0:T(8,128)(2,1)S(1)} fusion(bf16[1024,1664]{1,0:T(8,128)(2,1)} %get-tuple-element.34, bf16[1024,1536]{1,0:T(8,128)(2,1)} %copy-done.9, f32[1536]{0:T(1024)S(1)} %copy-done.33, f32[1024]{0:T(1024)S(1)} %copy-done.38), kind=kOutput, calls=%fused_computation.2 | convolution fusion | flops 5243338752 | bytes 11675648 | tf_op jit(solution)/shard_map/dot_general | solution.py:24
  435.8 6.1 convolution_convert_fusion.4
  442.0 19.0 %collective-permute-start.46 = (f32[3,128]{1,0:T(4,128)S(1)}, f32[3,128]{1,0:T(4,128)S(1)}, u32[]{:S(2)}, u32[]{:S(2)}) collective-permute-start(f32[3,128]{1,0:T(4,128)S(1)} %add.328), channel_id=1, source_target_pairs={{0,1},{1,0},{2,3},{3,2},{4,5},{5,4},{6,7},{7,6},{8,9},{9,8},{10,11... | collective-permute-start | bytes 4616 | tf_op jit(solution)/shard_map/ppermute | solution.py:419
  471.8 7.2 %collective-permute-done.47 = f32[3,128]{1,0:T(4,128)S(1)} collective-permute-done((f32[3,128]{1,0:T(4,128)S(1)}, f32[3,128]{1,0:T(4,128)S(1)}, u32[]{:S(2)}, u32[]{:S(2)}) %collective-permute-start.47) | collective-permute-done | bytes 1568 | tf_op jit(solution)/shard_map/ppermute | solution.py:419
  480.5 4.3 collective-permute-start.54
  487.5 4.6 collective-permute-start.27
  492.1 10.7 %collective-permute-done.54 = bf16[1,2,192,1024]{3,2,1,0:T(8,128)(2,1)S(1)} collective-permute-done((bf16[1,2,192,1024]{3,2,1,0:T(8,128)(2,1)S(1)}, bf16[1,2,192,1024]{3,2,1,0:T(8,128)(2,1)S(1)}, u32[]{:S(2)}, u32[]{:S(2)}) %collective-permute-start.54) | collective-permute-done | bytes 786464 | tf_op jit(solution)/shard_map/ppermute | solution.py:433
  502.8 4.4 collective-permute-start.55
  512.3 7.3 %collective-permute-done.27 = bf16[256,1536]{1,0:T(8,128)(2,1)S(1)} collective-permute-done((bf16[256,1536]{1,0:T(8,128)(2,1)S(1)}, bf16[256,1536]{1,0:T(8,128)(2,1)S(1)}, u32[]{:S(2)}, u32[]{:S(2)}) %collective-permute-start.27) | collective-permute-done | bytes 786464 | tf_op jit(solution)/shard_map/ppermute | solution.py:457
  522.2 11.4 %collective-permute-done.55 = bf16[1,2,192,1024]{3,2,1,0:T(8,128)(2,1)S(1)} collective-permute-done((bf16[1,2,192,1024]{3,2,1,0:T(8,128)(2,1)S(1)}, bf16[1,2,192,1024]{3,2,1,0:T(8,128)(2,1)S(1)}, u32[]{:S(2)}, u32[]{:S(2)}) %collective-permute-start.55) | collective-permute-done | bytes 786464 | tf_op jit(solution)/shard_map/ppermute | solution.py:433
  533.6 4.4 collective-permute-start.28
  546.9 22.2 %collective-permute-done.56 = bf16[1,2,192,1024]{3,2,1,0:T(8,128)(2,1)S(1)} collective-permute-done((bf16[1,2,192,1024]{3,2,1,0:T(8,128)(2,1)S(1)}, bf16[1,2,192,1024]{3,2,1,0:T(8,128)(2,1)S(1)}, u32[]{:S(2)}, u32[]{:S(2)}) %collective-permute-start.56) | collective-permute-done | bytes 786464 | tf_op jit(solution)/shard_map/ppermute | solution.py:433
  570.9 5.8 collective-permute-start.37
  580.0 6.0 collective-permute-done.37
  586.0 5.4 collective-permute-start.38
  591.7 7.4 %spread.3 = (f32[192,8192]{1,0:T(8,128)}, f32[192,128]{1,0:T(8,128)S(1)}) custom-call(bf16[8,192,1024]{2,1,0:T(8,128)(2,1)S(1)} %bitcast.116, bf16[192,8192]{1,0:T(8,128)(2,1)S(1)} %copy-done.1), custom_call_target="tpu_custom_call" | custom-call | flops 3145728 | bytes 12582912 | tf_op jit(solution)/shard_map/spread/pallas_call | solution.py:384
  602.9 4.6 collective-permute-start.39
  610.9 5.5 collective-permute-done.41
  637.6 31.0 %all-reduce.2.cloned.1.call-done = bf16[192,1536]{1,0:T(8,128)(2,1)} async-done(((bf16[192,1536]{1,0:T(8,128)(2,1)}), bf16[192,1536]{1,0:T(8,128)(2,1)}) %all-reduce.2.cloned.1.call-update) | async-done | bytes 589840 | tf_op jit(solution)/shard_map/psum | solution.py:682
  (389 shorter events, 195.1 us)
Async XLA Ops:
  7.2 93.3 %all-gather.3.cloned.1.call-start = ((), (), s32[]{:S(2)}) async-start(), calls=%async_computation.3 | async-start | bytes 5750784 | tf_op jit(solution)/shard_map/all_gather | solution.py:586
  15.3 136.4 %all-gather.5.cloned.1.call-start = ((), (), s32[]{:S(2)}) async-start(), calls=%async_computation.4 | async-start | bytes 5308416 | tf_op jit(solution)/shard_map/all_gather | solution.py:589
  22.4 23.7 %collective-permute-start.3 = (bf16[256,1536]{1,0:T(8,128)(2,1)S(1)}, bf16[256,1536]{1,0:T(8,128)(2,1)}, u32[]{:S(2)}, u32[]{:S(2)}) collective-permute-start(bf16[256,1536]{1,0:T(8,128)(2,1)S(1)} %copy-done.4), channel_id=1, source_target_pairs={{1,0},{2,1},{3,2},{5,4},{6,5},{7,6},{9,8},{10,9},{11,10},{13,12},{... | collective-permute-start | bytes 2359304 | tf_op jit(solution)/shard_map/ppermute | solution.py:434
  23.7 23.7 %collective-permute-start.9 = (bf16[192,2048]{1,0:T(8,128)(2,1)S(1)}, bf16[192,2048]{1,0:T(8,128)(2,1)S(1)}, u32[]{:S(2)}, u32[]{:S(2)}) collective-permute-start(bf16[192,2048]{1,0:T(8,128)(2,1)S(1)} %get-tuple-element.29), channel_id=1, source_target_pairs={{0,4},{4,0},{8,12},{12,8},{16,20},{20,16},{24,28},{28,24},{1,5},{5... | collective-permute-start | bytes 2359304 | tf_op jit(solution)/shard_map/ppermute | solution.py:419
  43.0 31.7 %collective-permute-start.15 = (bf16[256,1536]{1,0:T(8,128)(2,1)S(1)}, bf16[256,1536]{1,0:T(8,128)(2,1)S(1)}, u32[]{:S(2)}, u32[]{:S(2)}) collective-permute-start(bf16[256,1536]{1,0:T(8,128)(2,1)S(1)} %pad_maximum_fusion.12), channel_id=1, source_target_pairs={{0,8},{4,12},{8,0},{12,4},{16,24},{20,28},{24,16},{28,20},{1,9},{5... | collective-permute-start | bytes 2359304 | tf_op jit(solution)/shard_map/ppermute | solution.py:419
  44.5 32.4 %collective-permute-start.17 = (bf16[256,1536]{1,0:T(8,128)(2,1)S(1)}, bf16[256,1536]{1,0:T(8,128)(2,1)S(1)}, u32[]{:S(2)}, u32[]{:S(2)}) collective-permute-start(bf16[256,1536]{1,0:T(8,128)(2,1)S(1)} %pad_maximum_fusion.12), channel_id=1, source_target_pairs={{0,16},{4,20},{8,24},{12,28},{16,0},{20,4},{24,8},{28,12},{1,17},{... | collective-permute-start | bytes 2359304 | tf_op jit(solution)/shard_map/ppermute | solution.py:419
  46.0 32.3 %collective-permute-start.4 = (bf16[256,1536]{1,0:T(8,128)(2,1)}, bf16[256,1536]{1,0:T(8,128)(2,1)S(1)}, u32[]{:S(2)}, u32[]{:S(2)}) collective-permute-start(bf16[256,1536]{1,0:T(8,128)(2,1)} %collective-permute-done.3), channel_id=1, source_target_pairs={{1,0},{2,1},{3,2},{5,4},{6,5},{7,6},{9,8},{10,9},{11,10},{13,12},{... | collective-permute-start | bytes 2359304 | tf_op jit(solution)/shard_map/ppermute | solution.py:434
  64.6 80.5 %collective-permute-start.10 = (bf16[384,2048]{1,0:T(8,128)(2,1)}, bf16[384,2048]{1,0:T(8,128)(2,1)}, u32[]{:S(2)}, u32[]{:S(2)}) collective-permute-start(bf16[384,2048]{1,0:T(8,128)(2,1)} %pad_maximum_fusion.5), channel_id=1, source_target_pairs={{0,8},{4,12},{8,0},{12,4},{16,24},{20,28},{24,16},{28,20},{1,9},{5... | collective-permute-start | bytes 4718600 | tf_op jit(solution)/shard_map/ppermute | solution.py:419
  74.7 74.0 %collective-permute-start.11 = (bf16[384,2048]{1,0:T(8,128)(2,1)}, bf16[384,2048]{1,0:T(8,128)(2,1)}, u32[]{:S(2)}, u32[]{:S(2)}) collective-permute-start(bf16[384,2048]{1,0:T(8,128)(2,1)} %pad_maximum_fusion.5), channel_id=1, source_target_pairs={{0,16},{4,20},{8,24},{12,28},{16,0},{20,4},{24,8},{28,12},{1,17},{... | collective-permute-start | bytes 4718600 | tf_op jit(solution)/shard_map/ppermute | solution.py:419
  76.9 60.2 %collective-permute-start.16 = (bf16[128,1536]{1,0:T(8,128)(2,1)}, bf16[128,1536]{1,0:T(8,128)(2,1)}, u32[]{:S(2)}, u32[]{:S(2)}) collective-permute-start(bf16[128,1536]{1,0:T(8,128)(2,1)} %slice.279), channel_id=1, source_target_pairs={{0,16},{4,20},{8,24},{12,28},{16,0},{20,4},{24,8},{28,12},{1,17},{... | collective-permute-start | bytes 1179656 | tf_op jit(solution)/shard_map/ppermute | solution.py:419
  78.3 59.8 %collective-permute-start.18 = (bf16[128,1536]{1,0:T(8,128)(2,1)}, bf16[128,1536]{1,0:T(8,128)(2,1)}, u32[]{:S(2)}, u32[]{:S(2)}) collective-permute-start(bf16[128,1536]{1,0:T(8,128)(2,1)} %slice.280), channel_id=1, source_target_pairs={{0,8},{4,12},{8,0},{12,4},{16,24},{20,28},{24,16},{28,20},{1,9},{5... | collective-permute-start | bytes 1179656 | tf_op jit(solution)/shard_map/ppermute | solution.py:419
  143.5 41.3 %collective-permute-start.21 = (bf16[256,1536]{1,0:T(8,128)(2,1)}, bf16[256,1536]{1,0:T(8,128)(2,1)}, u32[]{:S(2)}, u32[]{:S(2)}) collective-permute-start(bf16[256,1536]{1,0:T(8,128)(2,1)} %param.21), channel_id=1, source_target_pairs={{0,4},{4,0},{8,12},{12,8},{16,20},{20,16},{24,28},{28,24},{1,5},{5... | collective-permute-start | bytes 2359304 | tf_op jit(solution)/shard_map/ppermute | solution.py:419
  143.5 23.5 %collective-permute-start.22 = (bf16[256,1536]{1,0:T(8,128)(2,1)}, bf16[256,1536]{1,0:T(8,128)(2,1)}, u32[]{:S(2)}, u32[]{:S(2)}) collective-permute-start(bf16[256,1536]{1,0:T(8,128)(2,1)} %param.21), channel_id=1, source_target_pairs={{0,1},{1,0},{2,3},{3,2},{4,5},{5,4},{6,7},{7,6},{8,9},{9,8},{10,11... | collective-permute-start | bytes 2359304 | tf_op jit(solution)/shard_map/ppermute | solution.py:419
  150.7 32.6 %collective-permute-start.13 = (bf16[192,2048]{1,0:T(8,128)(2,1)}, bf16[192,2048]{1,0:T(8,128)(2,1)}, u32[]{:S(2)}, u32[]{:S(2)}) collective-permute-start(bf16[192,2048]{1,0:T(8,128)(2,1)} %slice.276), channel_id=1, source_target_pairs={{0,8},{4,12},{8,0},{12,4},{16,24},{20,28},{24,16},{28,20},{1,9},{5... | collective-permute-start | bytes 2359304 | tf_op jit(solution)/shard_map/ppermute | solution.py:419
  157.6 25.7 %collective-permute-start.7 = (bf16[256,1536]{1,0:T(8,128)(2,1)S(1)}, bf16[256,1536]{1,0:T(8,128)(2,1)S(1)}, u32[]{:S(2)}, u32[]{:S(2)}) collective-permute-start(bf16[256,1536]{1,0:T(8,128)(2,1)S(1)} %pad_maximum_fusion.11), channel_id=1, source_target_pairs={{0,1},{1,0},{2,3},{3,2},{4,5},{5,4},{6,7},{7,6},{8,9},{9,8},{10,11... | collective-permute-start | bytes 2359304 | tf_op jit(solution)/shard_map/ppermute | solution.py:419
  229.2 58.2 %collective-permute-start.24 = (bf16[512,1536]{1,0:T(8,128)(2,1)S(1)}, bf16[512,1536]{1,0:T(8,128)(2,1)}, u32[]{:S(2)}, u32[]{:S(2)}) collective-permute-start(bf16[512,1536]{1,0:T(8,128)(2,1)S(1)} %pad_maximum_fusion.7), channel_id=1, source_target_pairs={{0,4},{4,0},{8,12},{12,8},{16,20},{20,16},{24,28},{28,24},{1,5},{5... | collective-permute-start | bytes 4718600 | tf_op jit(solution)/shard_map/ppermute | solution.py:419
  230.8 62.0 %collective-permute-start.19 = (bf16[512,1536]{1,0:T(8,128)(2,1)}, bf16[512,1536]{1,0:T(8,128)(2,1)}, u32[]{:S(2)}, u32[]{:S(2)}) collective-permute-start(bf16[512,1536]{1,0:T(8,128)(2,1)} %pad_maximum_fusion.6), channel_id=1, source_target_pairs={{0,4},{4,0},{8,12},{12,8},{16,20},{20,16},{24,28},{28,24},{1,5},{5... | collective-permute-start | bytes 4718600 | tf_op jit(solution)/shard_map/ppermute | solution.py:419
  251.8 33.9 %collective-permute-start.63 = (bf16[256,1536]{1,0:T(8,128)(2,1)S(1)}, bf16[256,1536]{1,0:T(8,128)(2,1)S(1)}, u32[]{:S(2)}, u32[]{:S(2)}) collective-permute-start(bf16[256,1536]{1,0:T(8,128)(2,1)S(1)} %pad_maximum_fusion.14), channel_id=1, source_target_pairs={{0,16},{4,20},{8,24},{12,28},{16,0},{20,4},{24,8},{28,12},{1,17},{... | collective-permute-start | bytes 2359304 | tf_op jit(solution)/shard_map/ppermute | solution.py:419
  270.9 52.0 %collective-permute-start.51 = (bf16[384,2048]{1,0:T(8,128)(2,1)S(1)}, bf16[384,2048]{1,0:T(8,128)(2,1)S(1)}, u32[]{:S(2)}, u32[]{:S(2)}) collective-permute-start(bf16[384,2048]{1,0:T(8,128)(2,1)S(1)} %pad_maximum_fusion.9), channel_id=1, source_target_pairs={{0,16},{4,20},{8,24},{12,28},{16,0},{20,4},{24,8},{28,12},{1,17},{... | collective-permute-start | bytes 4718600 | tf_op jit(solution)/shard_map/ppermute | solution.py:419
  285.7 38.5 %collective-permute-start.49 = (bf16[384,2048]{1,0:T(8,128)(2,1)S(1)}, bf16[384,2048]{1,0:T(8,128)(2,1)S(1)}, u32[]{:S(2)}, u32[]{:S(2)}) collective-permute-start(bf16[384,2048]{1,0:T(8,128)(2,1)S(1)} %pad_maximum_fusion.8), channel_id=1, source_target_pairs={{0,8},{4,12},{8,0},{12,4},{16,24},{20,28},{24,16},{28,20},{1,9},{5... | collective-permute-start | bytes 4718600 | tf_op jit(solution)/shard_map/ppermute | solution.py:419
  288.7 37.4 %collective-permute-start.25 = (bf16[256,1536]{1,0:T(8,128)(2,1)S(1)}, bf16[256,1536]{1,0:T(8,128)(2,1)S(1)}, u32[]{:S(2)}, u32[]{:S(2)}) collective-permute-start(bf16[256,1536]{1,0:T(8,128)(2,1)S(1)} %add_convert_fusion.8), channel_id=1, source_target_pairs={{0,1},{1,0},{2,3},{3,2},{4,5},{5,4},{6,7},{7,6},{8,9},{9,8},{10,11... | collective-permute-start | bytes 2359304 | tf_op jit(solution)/shard_map/ppermute | solution.py:419
  289.3 25.8 %collective-permute-start.65 = (bf16[2,64,1536]{2,1,0:T(8,128)(2,1)S(1)}, bf16[2,64,1536]{2,1,0:T(8,128)(2,1)S(1)}, u32[]{:S(2)}, u32[]{:S(2)}) collective-permute-start(bf16[2,64,1536]{2,1,0:T(8,128)(2,1)S(1)} %broadcast_select_fusion.11), channel_id=1, source_target_pairs={{0,2},{1,3},{2,0},{3,1},{4,6},{5,7},{6,4},{7,5},{8,10},{9,11},{10,... | collective-permute-start | bytes 1179656 | tf_op jit(solution)/shard_map/ppermute | solution.py:419
  294.2 40.2 %collective-permute-start.20 = (bf16[256,1536]{1,0:T(8,128)(2,1)S(1)}, bf16[256,1536]{1,0:T(8,128)(2,1)S(1)}, u32[]{:S(2)}, u32[]{:S(2)}) collective-permute-start(bf16[256,1536]{1,0:T(8,128)(2,1)S(1)} %add_convert_fusion.10), channel_id=1, source_target_pairs={{0,1},{1,0},{2,3},{3,2},{4,5},{5,4},{6,7},{7,6},{8,9},{9,8},{10,11... | collective-permute-start | bytes 2359304 | tf_op jit(solution)/shard_map/ppermute | solution.py:419
  316.0 28.3 %collective-permute-start.66 = (bf16[1,2,64,1536]{3,2,1,0:T(8,128)(2,1)}, bf16[1,2,64,1536]{3,2,1,0:T(8,128)(2,1)}, u32[]{:S(2)}, u32[]{:S(2)}) collective-permute-start(bf16[1,2,64,1536]{3,2,1,0:T(8,128)(2,1)} %fusion.26), channel_id=1, source_target_pairs={{0,1},{1,2},{2,3},{4,5},{5,6},{6,7},{8,9},{9,10},{10,11},{12,13},{... | collective-permute-start | bytes 1179656 | tf_op jit(solution)/shard_map/ppermute | solution.py:433
  322.9 26.1 %collective-permute-start.69 = (bf16[1,2,64,1536]{3,2,1,0:T(8,128)(2,1)}, bf16[1,2,64,1536]{3,2,1,0:T(8,128)(2,1)}, u32[]{:S(2)}, u32[]{:S(2)}) collective-permute-start(bf16[1,2,64,1536]{3,2,1,0:T(8,128)(2,1)} %fusion.26), channel_id=1, source_target_pairs={{1,0},{2,1},{3,2},{5,4},{6,5},{7,6},{9,8},{10,9},{11,10},{13,12},{... | collective-permute-start | bytes 1179656 | tf_op jit(solution)/shard_map/ppermute | solution.py:434
  326.1 48.6 %collective-permute-start.52 = (bf16[192,2048]{1,0:T(8,128)(2,1)}, bf16[192,2048]{1,0:T(8,128)(2,1)}, u32[]{:S(2)}, u32[]{:S(2)}) collective-permute-start(bf16[192,2048]{1,0:T(8,128)(2,1)} %constant_dynamic-slice_fusion.3), channel_id=1, source_target_pairs={{0,4},{4,0},{8,12},{12,8},{16,20},{20,16},{24,28},{28,24},{1,5},{5... | collective-permute-start | bytes 2359304 | tf_op jit(solution)/shard_map/ppermute | solution.py:419
  339.8 52.0 %all-to-all-start.1 = ((bf16[256,4,384]{2,0,1:T(8,128)(2,1)}), bf16[256,4,384]{2,0,1:T(8,128)(2,1)S(1)}, u32[]{:S(2)}, u32[]{:S(2)}) async-start(bf16[256,4,384]{2,0,1:T(8,128)(2,1)} %bitcast.125), calls=%async_computation.1 | async-start | bytes 1572864 | tf_op jit(solution)/shard_map/all_to_all | solution.py:646
  344.3 285.8 %reduce-scatter.2.cloned.1.call-start = ((), (), s32[]{:S(2)}) async-start(), calls=%async_computation.5 | async-start | bytes 5308416 | tf_op jit(solution)/shard_map/reduce_scatter | solution.py:681
  349.0 24.0 %collective-permute-start.70 = (bf16[1,2,64,1536]{3,2,1,0:T(8,128)(2,1)}, bf16[1,2,64,1536]{3,2,1,0:T(8,128)(2,1)}, u32[]{:S(2)}, u32[]{:S(2)}) collective-permute-start(bf16[1,2,64,1536]{3,2,1,0:T(8,128)(2,1)} %collective-permute-done.69), channel_id=1, source_target_pairs={{1,0},{2,1},{3,2},{5,4},{6,5},{7,6},{9,8},{10,9},{11,10},{13,12},{... | collective-permute-start | bytes 1179656 | tf_op jit(solution)/shard_map/ppermute | solution.py:434
  355.5 313.0 %all-reduce.2.cloned.1.call-start = ((), (), s32[]{:S(2)}) async-start(), calls=%async_computation.6 | async-start | bytes 1179648 | tf_op jit(solution)/shard_map/psum | solution.py:682
  377.7 101.3 %collective-permute-start.53 = (bf16[2,192,1024]{2,1,0:T(8,128)(2,1)}, bf16[2,192,1024]{2,1,0:T(8,128)(2,1)}, u32[]{:S(2)}, u32[]{:S(2)}) collective-permute-start(bf16[2,192,1024]{2,1,0:T(8,128)(2,1)} %broadcast_select_fusion), channel_id=1, source_target_pairs={{0,2},{1,3},{2,0},{3,1},{4,6},{5,7},{6,4},{7,5},{8,10},{9,11},{10,... | collective-permute-start | bytes 2359304 | tf_op jit(solution)/shard_map/ppermute | solution.py:419
  433.3 75.2 %collective-permute-start.32 = (bf16[4,192,1664]{2,1,0:T(8,128)(2,1)S(1)}, bf16[4,192,1664]{2,1,0:T(8,128)(2,1)S(1)}, u32[]{:S(2)}, u32[]{:S(2)}) collective-permute-start(bf16[4,192,1664]{2,1,0:T(8,128)(2,1)S(1)} %dynamic-slice_bitcast_fusion), channel_id=1, source_target_pairs={{0,4},{4,0},{8,12},{12,8},{16,20},{20,16},{24,28},{28,24},{1,5},{5... | collective-permute-start | bytes 7667720 | tf_op jit(solution)/shard_map/ppermute | solution.py:419
  461.1 26.2 %collective-permute-start.26 = (bf16[256,1536]{1,0:T(8,128)(2,1)S(1)}, bf16[256,1536]{1,0:T(8,128)(2,1)S(1)}, u32[]{:S(2)}, u32[]{:S(2)}) collective-permute-start(bf16[256,1536]{1,0:T(8,128)(2,1)S(1)} %get-tuple-element.64), channel_id=1, source_target_pairs={{0,1},{1,2},{2,3},{4,5},{5,6},{6,7},{8,9},{9,10},{10,11},{12,13},{... | collective-permute-start | bytes 2359304 | tf_op jit(solution)/shard_map/ppermute | solution.py:457
  470.5 40.5 %collective-permute-start.29 = (bf16[256,1536]{1,0:T(8,128)(2,1)S(1)}, bf16[256,1536]{1,0:T(8,128)(2,1)S(1)}, u32[]{:S(2)}, u32[]{:S(2)}) collective-permute-start(bf16[256,1536]{1,0:T(8,128)(2,1)S(1)} %get-tuple-element.65), channel_id=1, source_target_pairs={{1,0},{2,1},{3,2},{5,4},{6,5},{7,6},{9,8},{10,9},{11,10},{13,12},{... | collective-permute-start | bytes 2359304 | tf_op jit(solution)/shard_map/ppermute | solution.py:460
  484.9 22.4 %collective-permute-start.57 = (bf16[1,2,192,1024]{3,2,1,0:T(8,128)(2,1)S(1)}, bf16[1,2,192,1024]{3,2,1,0:T(8,128)(2,1)S(1)}, u32[]{:S(2)}, u32[]{:S(2)}) collective-permute-start(bf16[1,2,192,1024]{3,2,1,0:T(8,128)(2,1)S(1)} %fusion.18), channel_id=1, source_target_pairs={{1,0},{2,1},{3,2},{5,4},{6,5},{7,6},{9,8},{10,9},{11,10},{13,12},{... | collective-permute-start | bytes 2359304 | tf_op jit(solution)/shard_map/ppermute | solution.py:434
  487.5 32.1 %collective-permute-start.27 = (bf16[256,1536]{1,0:T(8,128)(2,1)S(1)}, bf16[256,1536]{1,0:T(8,128)(2,1)S(1)}, u32[]{:S(2)}, u32[]{:S(2)}) collective-permute-start(bf16[256,1536]{1,0:T(8,128)(2,1)S(1)} %add_convert_fusion.7), channel_id=1, source_target_pairs={{0,1},{1,2},{2,3},{4,5},{5,6},{6,7},{8,9},{9,10},{10,11},{12,13},{... | collective-permute-start | bytes 2359304 | tf_op jit(solution)/shard_map/ppermute | solution.py:457
  502.8 30.8 %collective-permute-start.55 = (bf16[1,2,192,1024]{3,2,1,0:T(8,128)(2,1)S(1)}, bf16[1,2,192,1024]{3,2,1,0:T(8,128)(2,1)S(1)}, u32[]{:S(2)}, u32[]{:S(2)}) collective-permute-start(bf16[1,2,192,1024]{3,2,1,0:T(8,128)(2,1)S(1)} %collective-permute-done.54), channel_id=1, source_target_pairs={{0,1},{1,2},{2,3},{4,5},{5,6},{6,7},{8,9},{9,10},{10,11},{12,13},{... | collective-permute-start | bytes 2359304 | tf_op jit(solution)/shard_map/ppermute | solution.py:433
  507.2 30.8 %collective-permute-start.58 = (bf16[1,2,192,1024]{3,2,1,0:T(8,128)(2,1)S(1)}, bf16[1,2,192,1024]{3,2,1,0:T(8,128)(2,1)S(1)}, u32[]{:S(2)}, u32[]{:S(2)}) collective-permute-start(bf16[1,2,192,1024]{3,2,1,0:T(8,128)(2,1)S(1)} %collective-permute-done.57), channel_id=1, source_target_pairs={{1,0},{2,1},{3,2},{5,4},{6,5},{7,6},{9,8},{10,9},{11,10},{13,12},{... | collective-permute-start | bytes 2359304 | tf_op jit(solution)/shard_map/ppermute | solution.py:434
  509.3 31.9 %collective-permute-start.33 = (bf16[96,1664]{1,0:T(8,128)(2,1)S(1)}, bf16[96,1664]{1,0:T(8,128)(2,1)S(1)}, u32[]{:S(2)}, u32[]{:S(2)}) collective-permute-start(bf16[96,1664]{1,0:T(8,128)(2,1)S(1)} %get-tuple-element.75), channel_id=1, source_target_pairs={{0,16},{4,20},{8,24},{12,28},{16,0},{20,4},{24,8},{28,12},{1,17},{... | collective-permute-start | bytes 958472 | tf_op jit(solution)/shard_map/ppermute | solution.py:419
  511.0 31.5 %collective-permute-start.35 = (bf16[96,1664]{1,0:T(8,128)(2,1)S(1)}, bf16[96,1664]{1,0:T(8,128)(2,1)S(1)}, u32[]{:S(2)}, u32[]{:S(2)}) collective-permute-start(bf16[96,1664]{1,0:T(8,128)(2,1)S(1)} %get-tuple-element.77), channel_id=1, source_target_pairs={{0,8},{4,12},{8,0},{12,4},{16,24},{20,28},{24,16},{28,20},{1,9},{5... | collective-permute-start | bytes 958472 | tf_op jit(solution)/shard_map/ppermute | solution.py:419
  520.9 23.5 %collective-permute-start.30 = (bf16[256,1536]{1,0:T(8,128)(2,1)S(1)}, bf16[256,1536]{1,0:T(8,128)(2,1)S(1)}, u32[]{:S(2)}, u32[]{:S(2)}) collective-permute-start(bf16[256,1536]{1,0:T(8,128)(2,1)S(1)} %get-tuple-element.63), channel_id=1, source_target_pairs={{1,0},{2,1},{3,2},{5,4},{6,5},{7,6},{9,8},{10,9},{11,10},{13,12},{... | collective-permute-start | bytes 2359304 | tf_op jit(solution)/shard_map/ppermute | solution.py:460
  533.6 66.3 %collective-permute-start.28 = (bf16[256,1536]{1,0:T(8,128)(2,1)}, bf16[256,1536]{1,0:T(8,128)(2,1)S(1)}, u32[]{:S(2)}, u32[]{:S(2)}) collective-permute-start(bf16[256,1536]{1,0:T(8,128)(2,1)} %get-tuple-element.62), channel_id=1, source_target_pairs={{0,1},{1,2},{2,3},{4,5},{5,6},{6,7},{8,9},{9,10},{10,11},{12,13},{... | collective-permute-start | bytes 2359304 | tf_op jit(solution)/shard_map/ppermute | solution.py:457
  538.0 31.1 %collective-permute-start.56 = (bf16[1,2,192,1024]{3,2,1,0:T(8,128)(2,1)S(1)}, bf16[1,2,192,1024]{3,2,1,0:T(8,128)(2,1)S(1)}, u32[]{:S(2)}, u32[]{:S(2)}) collective-permute-start(bf16[1,2,192,1024]{3,2,1,0:T(8,128)(2,1)S(1)} %collective-permute-done.55), channel_id=1, source_target_pairs={{0,1},{1,2},{2,3},{4,5},{5,6},{6,7},{8,9},{9,10},{10,11},{12,13},{... | collective-permute-start | bytes 2359304 | tf_op jit(solution)/shard_map/ppermute | solution.py:433
  541.2 37.1 %collective-permute-start.59 = (bf16[1,2,192,1024]{3,2,1,0:T(8,128)(2,1)S(1)}, bf16[1,2,192,1024]{3,2,1,0:T(8,128)(2,1)S(1)}, u32[]{:S(2)}, u32[]{:S(2)}) collective-permute-start(bf16[1,2,192,1024]{3,2,1,0:T(8,128)(2,1)S(1)} %collective-permute-done.58), channel_id=1, source_target_pairs={{1,0},{2,1},{3,2},{5,4},{6,5},{7,6},{9,8},{10,9},{11,10},{13,12},{... | collective-permute-start | bytes 2359304 | tf_op jit(solution)/shard_map/ppermute | solution.py:434
  542.8 27.8 %collective-permute-start.36 = (bf16[192,1664]{1,0:T(8,128)(2,1)S(1)}, bf16[192,1664]{1,0:T(8,128)(2,1)S(1)}, u32[]{:S(2)}, u32[]{:S(2)}) collective-permute-start(bf16[192,1664]{1,0:T(8,128)(2,1)S(1)} %pad_maximum_fusion.16), channel_id=1, source_target_pairs={{0,16},{4,20},{8,24},{12,28},{16,0},{20,4},{24,8},{28,12},{1,17},{... | collective-permute-start | bytes 1916936 | tf_op jit(solution)/shard_map/ppermute | solution.py:419
  544.5 26.1 %collective-permute-start.34 = (bf16[192,1664]{1,0:T(8,128)(2,1)S(1)}, bf16[192,1664]{1,0:T(8,128)(2,1)S(1)}, u32[]{:S(2)}, u32[]{:S(2)}) collective-permute-start(bf16[192,1664]{1,0:T(8,128)(2,1)S(1)} %pad_maximum_fusion.15), channel_id=1, source_target_pairs={{0,8},{4,12},{8,0},{12,4},{16,24},{20,28},{24,16},{28,20},{1,9},{5... | collective-permute-start | bytes 1916936 | tf_op jit(solution)/shard_map/ppermute | solution.py:419
  569.1 30.7 %collective-permute-start.31 = (bf16[256,1536]{1,0:T(8,128)(2,1)}, bf16[256,1536]{1,0:T(8,128)(2,1)S(1)}, u32[]{:S(2)}, u32[]{:S(2)}) collective-permute-start(bf16[256,1536]{1,0:T(8,128)(2,1)} %add_convert_fusion.4), channel_id=1, source_target_pairs={{1,0},{2,1},{3,2},{5,4},{6,5},{7,6},{9,8},{10,9},{11,10},{13,12},{... | collective-permute-start | bytes 2359304 | tf_op jit(solution)/shard_map/ppermute | solution.py:460
  578.4 23.2 %collective-permute-start.40 = (bf16[1,192,1664]{2,1,0:T(8,128)(2,1)S(1)}, bf16[1,192,1664]{2,1,0:T(8,128)(2,1)}, u32[]{:S(2)}, u32[]{:S(2)}) collective-permute-start(bf16[1,192,1664]{2,1,0:T(8,128)(2,1)S(1)} %fusion.22), channel_id=1, source_target_pairs={{1,0},{2,1},{3,2},{5,4},{6,5},{7,6},{9,8},{10,9},{11,10},{13,12},{... | collective-permute-start | bytes 1916936 | tf_op jit(solution)/shard_map/ppermute | solution.py:434
  (85 other events, 1111.5 us)
Sparse Core Ops, SparseCore 0:
  15.4 55.4 all-gather.2
  72.8 59.1 all-gather.4
  355.7 54.8 reduce-scatter.1
  630.2 38.2 all-reduce.1
